TPU v7x, 256 devices: a whole 4x4x8 slice. The times are simulated.
256 devices in a mesh: gx: 8 (over z), gy: 4 (over x), gz: 8 (over y, core).
Axes of the slice: x: 4, y: 4, z: 8, core: 2. Of those that a mesh axis runs over, the one named last changes fastest.
Arguments:
- params: float32 [59, 524288], P(None, ('gx', 'gy', 'gz')), may hold values from -6 to 6
- gradients: float32 [59, 524288], P(None, ('gx', 'gy', 'gz')), may hold values from -80 to 80
- moment_one: float32 [59, 524288], P(None, ('gx', 'gy', 'gz')), may hold values from -4 to 4
- moment_two: float32 [59, 524288], P(None, ('gx', 'gy', 'gz')), may hold values from 0.01 to 1
- keep_mask: int32 [524288], P(('gx', 'gy', 'gz')), may hold values from 0 to 1, as said below
Outputs:
- new_params: float32 [59, 524288], P(None, ('gx', 'gy', 'gz'))
- new_moment_one: float32 [59, 524288], P(None, ('gx', 'gy', 'gz'))
- new_moment_two: float32 [59, 524288], P(None, ('gx', 'gy', 'gz'))
- grad_rms: float32 [], replicated
Inputs may be any that keep to these rules, and one draw needn't show every extreme that they name: `keep_mask`: exactly 32 of the blocks of 128 aligned columns hold no 1; every other block holds at least one.
All inputs are finite; a program needn't handle non-finite values.
Results may differ from a plain program's by a relative error of at most 0.000067.
Values sent between devices are 32-bit elements; how exact they have to be, the bound alone decides.
No kernel may reach another device: no remote copies, remote signals or barrier semaphores. Data moves between devices by JAX's collectives and lax.ppermute only.
A program may use at most 64 MiB of HBM per device.

v0:
```python
import jax
import jax.numpy as jnp
from jax import lax
from jax.sharding import Mesh
from jax.sharding import PartitionSpec as P

FEATURES = 59
BLOCK = 128
MOVES = 2
STEP = 10
GX_GY_GZ = ("gx", "gy", "gz_0", "gz_1")


beta_one = 0.9
beta_two = 0.999
learn_rate = 0.05
adam_eps = 1e-08
clip_rms = 1.0


def passed_along(block, axis, distance):
    devices = range(lax.axis_size(axis))
    route = [(i - distance, i) for i in devices if i - distance in devices]
    return lax.ppermute(block, axis, route)


def sent_to_all(x, axis):
    size = lax.axis_size(axis)
    return lax.all_to_all(jnp.broadcast_to(x[None], (size, *x.shape)), axis, 0, 0, tiled=True)


def joined_along(tiles, dim):
    lengths = list(tiles.shape[1:])
    lengths[dim] *= tiles.shape[0]
    return jnp.moveaxis(tiles, 0, dim).reshape(lengths)


def gather_axes(x, axes, dim):
    far, near = axes
    tiles = sent_to_all(sent_to_all(x, far), near)
    return joined_along(tiles.swapaxes(0, 1).reshape(-1, *x.shape), dim)


def adam_update(params, gradients, moment_one, moment_two, clip_factor):
    clipped = clip_factor * gradients
    first = beta_one * moment_one + (1.0 - beta_one) * clipped
    second = beta_two * moment_two + (1.0 - beta_two) * clipped * clipped
    correct_one = 1.0 - beta_one**STEP
    correct_two = 1.0 - beta_two**STEP
    updated = params - learn_rate * (first / correct_one) / (
        jnp.sqrt(second / correct_two) + adam_eps
    )
    return (updated, first, second)


def relocate(stacked, table, blocks_dev):
    members = stacked.shape[0]
    flat_data = stacked.reshape(members * FEATURES, blocks_dev, BLOCK)
    window = jnp.einsum("anr,nw->awr", flat_data, table, precision=lax.Precision.HIGHEST)
    result = window[:, MOVES * blocks_dev : (MOVES + 1) * blocks_dev]
    for distance in range(1, MOVES + 1):
        outgoing = window[:, (MOVES - distance) * blocks_dev : (MOVES - distance + 1) * blocks_dev]
        result = result + passed_along(outgoing, GX_GY_GZ, -distance)
    return result.reshape(members, FEATURES, blocks_dev * BLOCK)


def shards(params, gradients, moment_one, moment_two, keep_mask):
    row_count = params.shape[1]
    blocks_dev = row_count // BLOCK
    devices_all = lax.axis_size(GX_GY_GZ)
    my_index = lax.axis_index(GX_GY_GZ)
    local_square = jnp.sum(gradients * gradients)
    counts = jnp.sum(keep_mask.reshape(blocks_dev, BLOCK), axis=1)
    block_alive = (counts > 0).astype(jnp.int32)
    local_alive = jnp.sum(block_alive)
    squares_all, alive_all = (
        gather_axes(local_square[None], (("gx", "gy"), ("gz_0", "gz_1")), 0),
        gather_axes(local_alive[None], (("gx", "gy"), ("gz_0", "gz_1")), 0),
    )
    square_total = jnp.sum(squares_all)
    lower = jnp.arange(devices_all, dtype=jnp.int32) < my_index
    offset = jnp.sum(jnp.where(lower, alive_all, 0)).astype(jnp.int32)
    grad_rms = jnp.sqrt(square_total / (FEATURES * row_count * devices_all))
    clip_factor = jnp.minimum(1.0, clip_rms / (grad_rms + 1e-06))
    local_rank = jnp.cumsum(block_alive) - block_alive
    window_slot = offset + local_rank - (my_index - MOVES) * blocks_dev
    window_blocks = (MOVES + 1) * blocks_dev
    columns = jnp.arange(window_blocks, dtype=jnp.int32)[None, :]
    table = ((columns == window_slot[:, None]) & (block_alive[:, None] > 0)).astype(jnp.float32)
    kept_rows = keep_mask[None, None, :] > 0
    updated, first, second = adam_update(params, gradients, moment_one, moment_two, clip_factor)
    stacked = jnp.where(kept_rows, jnp.stack([updated, first, second]), 0.0)
    moved = relocate(stacked, table, blocks_dev)
    return (moved[0], moved[1], moved[2], grad_rms)


def solution(mesh):
    split = Mesh(
        mesh.devices.reshape(mesh.shape["gx"], mesh.shape["gy"], 4, 2), ("gx", "gy", "gz_0", "gz_1")
    )
    placed = (
        P(None, GX_GY_GZ),
        P(None, GX_GY_GZ),
        P(None, GX_GY_GZ),
        P(None, GX_GY_GZ),
        P(GX_GY_GZ),
    )
    return jax.shard_map(
        shards,
        mesh=split,
        in_specs=placed,
        out_specs=(P(None, GX_GY_GZ), P(None, GX_GY_GZ), P(None, GX_GY_GZ), P()),
        check_vma=False,
    )
```

profile of v0, /device:TPU:30, one launch (start us, length us, event | category | flops | bytes accessed | tf_op | source)
XLA Modules:
  0.0 119.9 jit_solution(8310974378242429334)
XLA Ops:
  0.6 1.8 %multiply_reduce_fusion = f32[]{:T(128)} fusion(f32[59,2048]{1,0:T(8,128)} %param.6), kind=kLoop, calls=%fused_computation.11 | loop fusion | flops 241663 | bytes 483332 | tf_op jit(solution)/shard_map/reduce_sum | solution.py:72
  2.4 1.3 %broadcast_in_dim.54 = f32[32,1,1]{2,1,0:T(1,128)} broadcast(f32[]{:T(128)} %multiply_reduce_fusion), dimensions={} | broadcast | bytes 132 | tf_op jit(solution)/shard_map/broadcast_in_dim | solution.py:29
  3.7 11.6 %all-to-all-start.2 = ((f32[32,1,1]{2,1,0:T(1,128)}), f32[32,1,1]{2,1,0:T(1,128)S(1)}, u32[]{:S(2)}, u32[]{:S(2)}) async-start(f32[32,1,1]{2,1,0:T(1,128)} %broadcast_in_dim.54), calls=%async_computation.2 | async-start | bytes 32768 | tf_op jit(solution)/shard_map/all_to_all | solution.py:29
  15.2 0.8 bitcast_reduce_fusion
  16.1 0.6 fusion.15
  16.7 0.7 compare_bitcast_fusion
  17.4 5.8 %all-to-all-done.2 = f32[32,1,1]{2,1,0:T(1,128)S(1)} async-done(((f32[32,1,1]{2,1,0:T(1,128)}), f32[32,1,1]{2,1,0:T(1,128)S(1)}, u32[]{:S(2)}, u32[]{:S(2)}) %all-to-all-start.2) | async-done | bytes 160 | tf_op jit(solution)/shard_map/all_to_all | solution.py:29
  23.1 1.3 %broadcast_in_dim.48 = s32[32,1,1]{2,1,0:T(1,128)} broadcast(s32[]{:T(128)} %fusion.15), dimensions={} | broadcast | bytes 132 | tf_op jit(solution)/shard_map/broadcast_in_dim | solution.py:29
  24.4 5.5 %all-to-all-start = ((s32[32,1,1]{2,1,0:T(1,128)}), s32[32,1,1]{2,1,0:T(1,128)S(1)}, u32[]{:S(2)}, u32[]{:S(2)}) async-start(s32[32,1,1]{2,1,0:T(1,128)} %broadcast_in_dim.48), calls=%async_computation | async-start | bytes 32768 | tf_op jit(solution)/shard_map/all_to_all | solution.py:29
  29.9 0.3 reduce.5
  30.3 7.7 %all-to-all-done = s32[32,1,1]{2,1,0:T(1,128)S(1)} async-done(((s32[32,1,1]{2,1,0:T(1,128)}), s32[32,1,1]{2,1,0:T(1,128)S(1)}, u32[]{:S(2)}, u32[]{:S(2)}) %all-to-all-start) | async-done | bytes 160 | tf_op jit(solution)/shard_map/all_to_all | solution.py:29
  37.9 0.6 broadcast_in_dim.56
  38.5 4.7 %all-to-all-start.3 = ((f32[8,32,1]{1,2,0:T(1,128)}), f32[8,32,1]{1,2,0:T(1,128)S(1)}, u32[]{:S(2)}, u32[]{:S(2)}) async-start(f32[8,32,1]{1,2,0:T(1,128)} %broadcast_in_dim.56), calls=%async_computation.3 | async-start | bytes 8192 | tf_op jit(solution)/shard_map/all_to_all | solution.py:29
  43.5 0.7 reduce.3
  44.1 2.2 %all-to-all-done.3 = f32[8,32,1]{1,2,0:T(1,128)S(1)} async-done(((f32[8,32,1]{1,2,0:T(1,128)}), f32[8,32,1]{1,2,0:T(1,128)S(1)}, u32[]{:S(2)}, u32[]{:S(2)}) %all-to-all-start.3) | async-done | bytes 1056 | tf_op jit(solution)/shard_map/all_to_all | solution.py:29
  46.4 0.6 broadcast_in_dim.50
  47.0 5.3 %all-to-all-start.1 = ((s32[8,32,1]{1,2,0:T(1,128)}), s32[8,32,1]{1,2,0:T(1,128)S(1)}, u32[]{:S(2)}, u32[]{:S(2)}) async-start(s32[8,32,1]{1,2,0:T(1,128)} %broadcast_in_dim.50), calls=%async_computation.1 | async-start | bytes 8192 | tf_op jit(solution)/shard_map/all_to_all | solution.py:29
  52.3 0.6 reduce_sum.49
  53.6 1.9 %subtract_bitcast_fusion = (f32[1,59,2048]{2,1,0:T(8,128)S(1)}, f32[1,59,2048]{2,1,0:T(8,128)S(1)}, f32[1,59,2048]{2,1,0:T(8,128)S(1)}) fusion(f32[59,2048]{1,0:T(8,128)} %param.5, f32[59,2048]{1,0:T(8,128)} %param.6, f32[]{:T(128)S(6)} %min.3, f32[59,2048]{1,0:T(8,128)} %param.7, f32[59,2048]{1,0:T(8,128)} %param.8), kind=kLoop, calls=%fused_computation.9 | loop fusion | flops 1570816 | bytes 3383300 | tf_op jit(solution)/shard_map/stack | solution.py:92
  55.6 0.2 stack.18
  55.9 0.6 fusion.11
  56.5 0.7 add_subtract_fusion
  57.2 2.0 %convolution_bitcast_fusion = f32[177,48,128]{2,1,0:T(8,128)S(1)} fusion(f32[177,16,128]{2,1,0:T(8,128)S(1)} %stack.18, pred[16,128]{1,0:T(8,128)(4,1)S(1)} %compare_bitcast_fusion, s32[16]{0:T(128)S(1)} %add_subtract_fusion, pred[16]{0:T(512)(128)(4,1)S(1)} %get-tuple-element.12), kind=kOutput, calls=%fused_computation | convolution fusion | flops 209161728 | bytes 5802064 | tf_op jit(solution)/shard_map/anr,nw->awr/dot_general | solution.py:59
  59.2 0.2 fusion.16
  59.4 2.5 %collective-permute-start = (f32[177,16,128]{2,1,0:T(8,128)S(1)}, f32[177,16,128]{2,1,0:T(8,128)S(1)}, u32[]{:S(2)}, u32[]{:S(2)}) collective-permute-start(f32[177,16,128]{2,1,0:T(8,128)S(1)} %get-tuple-element.4), channel_id=1, source_target_pairs={{1,0},{2,1},{3,2},{4,3},{5,4},{6,5},{7,6},{8,7},{9,8},{10,9},{11,1... | collective-permute-start | bytes 4349960 | tf_op jit(solution)/shard_map/ppermute | solution.py:24
  61.8 2.5 %collective-permute-start.1 = (f32[177,16,128]{2,1,0:T(8,128)S(1)}, f32[177,16,128]{2,1,0:T(8,128)S(1)}, u32[]{:S(2)}, u32[]{:S(2)}) collective-permute-start(f32[177,16,128]{2,1,0:T(8,128)S(1)} %get-tuple-element.5), channel_id=1, source_target_pairs={{2,0},{3,1},{4,2},{5,3},{6,4},{7,5},{8,6},{9,7},{10,8},{11,9},{12,... | collective-permute-start | bytes 4349960 | tf_op jit(solution)/shard_map/ppermute | solution.py:24
  64.3 27.9 %collective-permute-done = f32[177,16,128]{2,1,0:T(8,128)S(1)} collective-permute-done((f32[177,16,128]{2,1,0:T(8,128)S(1)}, f32[177,16,128]{2,1,0:T(8,128)S(1)}, u32[]{:S(2)}, u32[]{:S(2)}) %collective-permute-start) | collective-permute-done | bytes 1450016 | tf_op jit(solution)/shard_map/ppermute | solution.py:24
  92.2 23.1 %collective-permute-done.1 = f32[177,16,128]{2,1,0:T(8,128)S(1)} collective-permute-done((f32[177,16,128]{2,1,0:T(8,128)S(1)}, f32[177,16,128]{2,1,0:T(8,128)S(1)}, u32[]{:S(2)}, u32[]{:S(2)}) %collective-permute-start.1) | collective-permute-done | bytes 1450016 | tf_op jit(solution)/shard_map/ppermute | solution.py:24
  115.4 0.3 fusion
  115.8 1.0 copy.16
  116.8 1.0 copy.15
  117.8 1.0 copy.14
  (10 shorter events, 0.6 us)
Async XLA Ops:
  3.7 19.5 %all-to-all-start.2 = ((f32[32,1,1]{2,1,0:T(1,128)}), f32[32,1,1]{2,1,0:T(1,128)S(1)}, u32[]{:S(2)}, u32[]{:S(2)}) async-start(f32[32,1,1]{2,1,0:T(1,128)} %broadcast_in_dim.54), calls=%async_computation.2 | async-start | bytes 32768 | tf_op jit(solution)/shard_map/all_to_all | solution.py:29
  24.4 13.5 %all-to-all-start = ((s32[32,1,1]{2,1,0:T(1,128)}), s32[32,1,1]{2,1,0:T(1,128)S(1)}, u32[]{:S(2)}, u32[]{:S(2)}) async-start(s32[32,1,1]{2,1,0:T(1,128)} %broadcast_in_dim.48), calls=%async_computation | async-start | bytes 32768 | tf_op jit(solution)/shard_map/all_to_all | solution.py:29
  38.5 7.8 %all-to-all-start.3 = ((f32[8,32,1]{1,2,0:T(1,128)}), f32[8,32,1]{1,2,0:T(1,128)S(1)}, u32[]{:S(2)}, u32[]{:S(2)}) async-start(f32[8,32,1]{1,2,0:T(1,128)} %broadcast_in_dim.56), calls=%async_computation.3 | async-start | bytes 8192 | tf_op jit(solution)/shard_map/all_to_all | solution.py:29
  47.0 8.9 %all-to-all-start.1 = ((s32[8,32,1]{1,2,0:T(1,128)}), s32[8,32,1]{1,2,0:T(1,128)S(1)}, u32[]{:S(2)}, u32[]{:S(2)}) async-start(s32[8,32,1]{1,2,0:T(1,128)} %broadcast_in_dim.50), calls=%async_computation.1 | async-start | bytes 8192 | tf_op jit(solution)/shard_map/all_to_all | solution.py:29
  59.4 32.9 %collective-permute-start = (f32[177,16,128]{2,1,0:T(8,128)S(1)}, f32[177,16,128]{2,1,0:T(8,128)S(1)}, u32[]{:S(2)}, u32[]{:S(2)}) collective-permute-start(f32[177,16,128]{2,1,0:T(8,128)S(1)} %get-tuple-element.4), channel_id=1, source_target_pairs={{1,0},{2,1},{3,2},{4,3},{5,4},{6,5},{7,6},{8,7},{9,8},{10,9},{11,1... | collective-permute-start | bytes 4349960 | tf_op jit(solution)/shard_map/ppermute | solution.py:24
  61.8 53.5 %collective-permute-start.1 = (f32[177,16,128]{2,1,0:T(8,128)S(1)}, f32[177,16,128]{2,1,0:T(8,128)S(1)}, u32[]{:S(2)}, u32[]{:S(2)}) collective-permute-start(f32[177,16,128]{2,1,0:T(8,128)S(1)} %get-tuple-element.5), channel_id=1, source_target_pairs={{2,0},{3,1},{4,2},{5,3},{6,4},{7,5},{8,6},{9,7},{10,8},{11,9},{12,... | collective-permute-start | bytes 4349960 | tf_op jit(solution)/shard_map/ppermute | solution.py:24
where the time goes:
time: 120 us
  waiting for transfers between devices  66.7 us (56%)
  starting transfers between devices  32 us (27%)
  other arithmetic  9.26 us (8%)
  local copies, waits for them, and re-layouts  7.27 us (6%)
  between operations  2.63 us (2%)
  matrix products  1.97 us (2%)
    ppermute x2, waiting for transfers between devices, passed_along(): return lax.ppermute(block, axis, route)  51.1 us
    all_to_all x4, starting transfers between devices, sent_to_all(): lax.all_to_all(jnp.broadcast_to(x[None], (size, *x.shape)), axis, 0, 0, t...  27.1 us
    all_to_all x4, waiting for transfers between devices, sent_to_all(): lax.all_to_all(jnp.broadcast_to(x[None], (size, *x.shape)), axis, 0, 0, t...  15.7 us
    ppermute x2, starting transfers between devices, passed_along(): return lax.ppermute(block, axis, route)  4.94 us
    broadcast_in_dim x4, local copies, waits for them, and re-layouts, sent_to_all(): jnp.broadcast_to(x[None], (size, *x.shape))  3.71 us
    unnamed x6, local copies, waits for them, and re-layouts  2.97 us
  transfers between devices with their start and end apart: 6, of which 5 were waited for; matrix products, arithmetic and copies ran while one was open for 5% of the time, Pallas kernels for 0%

commit v1 on v0

v1 whole, which is shorter than its diff:
```python
import functools

import jax
import jax.numpy as jnp
from jax import lax
from jax.experimental import pallas as pl
from jax.experimental.pallas import tpu as pltpu
from jax.sharding import Mesh
from jax.sharding import PartitionSpec as P

FEATURES = 59
BLOCK = 128
STEP = 10
AXES = ("gx", "gy", "gz_0", "gz_1")

beta_one = 0.9
beta_two = 0.999
learn_rate = 0.05
adam_eps = 1e-08
clip_rms = 1.0
correct_one = 1.0 - beta_one**STEP
correct_two = 1.0 - beta_two**STEP


def from_next_chip(x):
    size = lax.axis_size(AXES)
    return lax.ppermute(x, AXES, [(i, i - 2) for i in range(2, size)])


def swap_cores(x):
    return lax.ppermute(x, "gz_1", [(0, 1), (1, 0)])


def sent_to_all(x, axes):
    size = lax.axis_size(axes)
    return lax.all_to_all(jnp.broadcast_to(x[None], (size, *x.shape)), axes, 0, 0, tiled=True)


def final_kernel(index, valid, po, ps, pr, vo, vs, vr, mo, ms, mr, p_out, m_out, v_out):
    for slot in range(p_out.shape[1] // BLOCK):
        place = index[slot]
        part = place // 16
        lanes = pl.ds(pl.multiple_of((place % 16) * BLOCK, BLOCK), BLOCK)
        here = pl.ds(slot * BLOCK, BLOCK)

        def pick(own, swapped, received):
            later = jnp.where(part == 1, swapped[:, lanes], received[:, lanes])
            return jnp.where(valid[slot] > 0, jnp.where(part == 0, own[:, lanes], later), 0.0)

        first = pick(mo, ms, mr)
        second = pick(vo, vs, vr)
        m_out[:, here] = first
        v_out[:, here] = second
        p_out[:, here] = pick(po, ps, pr) - learn_rate * (first / correct_one) / (
            jnp.sqrt(second / correct_two) + adam_eps
        )


def shards(params, gradients, moment_one, moment_two, keep_mask):
    rows = params.shape[1]
    blocks = rows // BLOCK
    devices = lax.axis_size(AXES)
    core = lax.axis_index("gz_1")
    kept = keep_mask[None, :] > 0

    alive = (jnp.max(keep_mask.reshape(blocks, BLOCK), axis=1) > 0).astype(jnp.int32)
    pair = jnp.stack([jnp.sum(gradients * gradients), jnp.sum(alive).astype(jnp.float32)])
    near = ("gz_0", "gz_1")
    far = ("gx", "gy")
    near_pairs = sent_to_all(pair, near)
    near_lower = jnp.arange(8) < lax.axis_index(near)
    far_pairs = sent_to_all(jnp.sum(near_pairs, axis=0), far)
    far_lower = jnp.arange(32) < lax.axis_index(far)
    lower = jnp.sum(jnp.where(near_lower, near_pairs[:, 1], 0.0)) + jnp.sum(
        jnp.where(far_lower, far_pairs[:, 1], 0.0)
    )
    offset = lower.astype(jnp.int32)
    grad_rms = jnp.sqrt(jnp.sum(far_pairs[:, 0]) / (FEATURES * rows * devices))
    clip_factor = jnp.minimum(1.0, clip_rms / (grad_rms + 1e-06))

    def window(own):
        received = from_next_chip(own)
        swapped = swap_cores(jnp.where(core == 0, received, own))
        return own, swapped, received

    p_window = window(jnp.where(kept, params, 0.0))
    clipped = clip_factor * gradients
    first = jnp.where(kept, beta_one * moment_one + (1.0 - beta_one) * clipped, 0.0)
    second = jnp.where(
        kept, beta_two * moment_two + (1.0 - beta_two) * clipped * clipped, 0.0
    )
    v_window = window(second)
    m_window = window(first)

    def alive_in(x):
        return (jnp.max(x[0].reshape(blocks, BLOCK), axis=1) > 0).astype(jnp.int32)

    flags = jnp.concatenate([alive, alive_in(v_window[1]), alive_in(v_window[2])])
    place = jnp.arange(3 * blocks)
    rank = jnp.sum(jnp.where(place[:, None] < place[None, :], flags[:, None], 0), axis=0)
    wanted = lax.axis_index(AXES) * blocks - offset + jnp.arange(blocks)
    match = (rank[None, :] == wanted[:, None]) & (flags[None, :] > 0)
    index = jnp.sum(jnp.where(match, place[None, :], 0), axis=1)
    valid = jnp.sum(match.astype(jnp.int32), axis=1)

    smem = pl.BlockSpec(memory_space=pltpu.SMEM)
    vmem = pl.BlockSpec(memory_space=pltpu.VMEM)
    out = jax.ShapeDtypeStruct(params.shape, jnp.float32)
    p1, m1, v1 = pl.pallas_call(
        final_kernel,
        out_shape=(out, out, out),
        in_specs=[smem, smem] + [vmem] * 9,
        out_specs=(vmem, vmem, vmem),
        name="compact",
    )(index, valid, *p_window, *v_window, *m_window)
    return p1, m1, v1, grad_rms


def solution(mesh):
    split = Mesh(
        mesh.devices.reshape(mesh.shape["gx"], mesh.shape["gy"], 4, 2), AXES
    )
    spec = P(None, AXES)
    return jax.shard_map(
        shards,
        mesh=split,
        in_specs=(spec, spec, spec, spec, P(AXES)),
        out_specs=(spec, spec, spec, P()),
        check_vma=False,
    )
```

time: 120 us -> 87.1 us (0.73)
  waiting for transfers between devices: 66.7 us -> 38.8 us
  starting transfers between devices: 32 us -> 25.5 us
  local copies, waits for them, and re-layouts: 7.27 us -> 2.98 us
  Pallas kernels: 0 us -> 4.02 us
  between operations: 2.63 us -> 4.63 us
  matrix products: 1.97 us -> 0 us
  other arithmetic: 9.26 us -> 10.5 us
    ppermute x2 -> x6, waiting for transfers between devices: 51.1 us -> 27.8 us  [the longest x3 27.1 us: from_next_chip(): return lax.ppermute(x, AXES, [(i, i - 2) for i in range(2, size)])]
    all_to_all x4 -> x2, starting transfers between devices: 27.1 us -> 16.2 us  [sent_to_all(): lax.all_to_all(jnp.broadcast_to(x[None], (size, *x.shape)), axes, 0, 0, t...]
    all_to_all x4 -> x2, waiting for transfers between devices: 15.7 us -> 11 us  [sent_to_all(): lax.all_to_all(jnp.broadcast_to(x[None], (size, *x.shape)), axes, 0, 0, t...]
    ppermute x2 -> x6, starting transfers between devices: 4.94 us -> 9.22 us  [the longest x3 9.21 us: from_next_chip(): return lax.ppermute(x, AXES, [(i, i - 2) for i in range(2, size)])]
    pallas_call x0 -> x1, Pallas kernels: none -> 4.02 us  [shards(): pl.pallas_call(final_kernel, out_shape=(out, out, out), in_specs=[smem, s...]
    select_n x0 -> x4, other arithmetic: none -> 3.46 us  [the longest x3 1.87 us: window(): swapped = swap_cores(jnp.where(core == 0, received, own))]
    broadcast_in_dim x4 -> x2, local copies, waits for them, and re-layouts: 3.71 us -> 1.21 us  [sent_to_all(): jnp.broadcast_to(x[None], (size, *x.shape))]
    dot_general x1 -> x0, matrix products: 1.97 us -> none  [relocate(): jnp.einsum('anr,nw->awr', flat_data, table, precision=lax.Precision.HIGHEST)]
  transfers between devices with their start and end apart: 6 -> 8, of which waited for: 5 -> 6; matrix products, arithmetic and copies ran while one was open for 5% -> 5% of each run, Pallas kernels for 0% -> 0%
where the time goes in v1:
time: 87.1 us; the launch traced here: 86.4 us
  waiting for transfers between devices  38.8 us (45%)
  starting transfers between devices  25.5 us (29%)
  other arithmetic  10.5 us (12%)
  between operations  4.63 us (5%)
  Pallas kernels  4.02 us (5%)
  local copies, waits for them, and re-layouts  2.98 us (3%)
    ppermute x3, waiting for transfers between devices, from_next_chip(): return lax.ppermute(x, AXES, [(i, i - 2) for i in range(2, size)])  27.1 us
    all_to_all x2, starting transfers between devices, sent_to_all(): lax.all_to_all(jnp.broadcast_to(x[None], (size, *x.shape)), axes, 0, 0, t...  16.2 us
    all_to_all x2, waiting for transfers between devices, sent_to_all(): lax.all_to_all(jnp.broadcast_to(x[None], (size, *x.shape)), axes, 0, 0, t...  11 us
    ppermute x3, starting transfers between devices, from_next_chip(): return lax.ppermute(x, AXES, [(i, i - 2) for i in range(2, size)])  9.21 us
    pallas_call x1, Pallas kernels, shards(): pl.pallas_call(final_kernel, out_shape=(out, out, out), in_specs=[smem, s...  4.02 us
    select_n x3, other arithmetic, window(): swapped = swap_cores(jnp.where(core == 0, received, own))  1.87 us
    reduce_sum x1, other arithmetic, shards(): jnp.sum(gradients * gradients)  1.84 us
  transfers between devices with their start and end apart: 8, of which 6 were waited for; matrix products, arithmetic and copies ran while one was open for 5% of the time, Pallas kernels for 0%

profile of v1, /device:TPU:30, one launch (start us, length us, event | category | flops | bytes accessed | tf_op | source)
XLA Modules:
  0.0 86.4 jit_solution(5119317758348539509)
XLA Ops:
  0.6 1.8 %multiply_reduce_fusion = f32[]{:T(128)} fusion(f32[59,2048]{1,0:T(8,128)} %param.6), kind=kLoop, calls=%fused_computation.4 | loop fusion | flops 241663 | bytes 483332 | tf_op jit(solution)/shard_map/reduce_sum | solution.py:67
  2.5 0.8 bitcast_reduce_fusion
  3.3 0.6 fusion.4
  4.6 0.7 pad_maximum_fusion
  5.3 0.6 broadcast_in_dim.73
  5.9 4.7 %all-to-all-start = ((f32[8,1,2]{2,1,0:T(1,128)}), f32[8,1,2]{2,1,0:T(1,128)S(1)}, u32[]{:S(2)}, u32[]{:S(2)}) async-start(f32[8,1,2]{2,1,0:T(1,128)} %broadcast_in_dim.73), calls=%async_computation | async-start | bytes 8192 | tf_op jit(solution)/shard_map/all_to_all | solution.py:36
  10.6 3.1 %all-to-all-done = f32[8,1,2]{2,1,0:T(1,128)S(1)} async-done(((f32[8,1,2]{2,1,0:T(1,128)}), f32[8,1,2]{2,1,0:T(1,128)S(1)}, u32[]{:S(2)}, u32[]{:S(2)}) %all-to-all-start) | async-done | bytes 96 | tf_op jit(solution)/shard_map/all_to_all | solution.py:36
  13.8 0.6 broadcast_in_dim.74
  14.4 11.6 %all-to-all-start.1 = ((f32[32,1,2]{2,1,0:T(1,128)}), f32[32,1,2]{2,1,0:T(1,128)S(1)}, u32[]{:S(2)}, u32[]{:S(2)}) async-start(f32[32,1,2]{2,1,0:T(1,128)} %broadcast_in_dim.74), calls=%async_computation.1 | async-start | bytes 32768 | tf_op jit(solution)/shard_map/all_to_all | solution.py:36
  26.0 7.9 %all-to-all-done.1 = f32[32,1,2]{2,1,0:T(1,128)S(1)} async-done(((f32[32,1,2]{2,1,0:T(1,128)}), f32[32,1,2]{2,1,0:T(1,128)S(1)}, u32[]{:S(2)}, u32[]{:S(2)}) %all-to-all-start.1) | async-done | bytes 288 | tf_op jit(solution)/shard_map/all_to_all | solution.py:36
  33.9 0.6 slice_reduce_fusion
  35.3 1.6 %add_select_fusion = (f32[59,2048]{1,0:T(8,128)S(1)}, f32[59,2048]{1,0:T(8,128)S(1)}, f32[59,2048]{1,0:T(8,128)S(1)}) fusion(f32[59,2048]{1,0:T(8,128)} %param.7, f32[59,2048]{1,0:T(8,128)S(1)} %copy-done.4, f32[]{:T(128)S(6)} %min.3, pred[2048]{0:T(1024)(128)(4,1)S(1)} %broadcast_compare_fusion, f32[59,2048]{1,0:T(8,128)} %param.8, f32[59,2048]{1,0:T(8,128)} %param.5), kind=kLoop, calls=%fused_computation.3 | loop fusion | flops 1329152 | bytes 3385348 | tf_op jit(solution)/shard_map/jit(_where)/select_n | solution.py:88
  36.9 2.5 %collective-permute-start.4 = (f32[59,2048]{1,0:T(8,128)S(1)}, f32[59,2048]{1,0:T(8,128)S(1)}, u32[]{:S(2)}, u32[]{:S(2)}) collective-permute-start(f32[59,2048]{1,0:T(8,128)S(1)} %get-tuple-element.14.mo), channel_id=1, source_target_pairs={{2,0},{3,1},{4,2},{5,3},{6,4},{7,5},{8,6},{9,7},{10,8},{11,9},{12,... | collective-permute-start | bytes 1449992 | tf_op jit(solution)/shard_map/ppermute | solution.py:27
  39.4 0.1 copy.12
  39.5 0.6 fusion.2
  40.1 0.6 fusion.3
  42.0 3.4 %collective-permute-start = (f32[59,2048]{1,0:T(8,128)S(1)}, f32[59,2048]{1,0:T(8,128)S(1)}, u32[]{:S(2)}, u32[]{:S(2)}) collective-permute-start(f32[59,2048]{1,0:T(8,128)S(1)} %get-tuple-element.15.vo), channel_id=1, source_target_pairs={{2,0},{3,1},{4,2},{5,3},{6,4},{7,5},{8,6},{9,7},{10,8},{11,9},{12,... | collective-permute-start | bytes 1449992 | tf_op jit(solution)/shard_map/ppermute | solution.py:27
  45.4 3.4 %collective-permute-start.2 = (f32[59,2048]{1,0:T(8,128)S(1)}, f32[59,2048]{1,0:T(8,128)S(1)}, u32[]{:S(2)}, u32[]{:S(2)}) collective-permute-start(f32[59,2048]{1,0:T(8,128)S(1)} %get-tuple-element.16.po), channel_id=1, source_target_pairs={{2,0},{3,1},{4,2},{5,3},{6,4},{7,5},{8,6},{9,7},{10,8},{11,9},{12,... | collective-permute-start | bytes 1449992 | tf_op jit(solution)/shard_map/ppermute | solution.py:27
  48.8 9.1 %collective-permute-done.4.mr = f32[59,2048]{1,0:T(8,128)S(1)} collective-permute-done((f32[59,2048]{1,0:T(8,128)S(1)}, f32[59,2048]{1,0:T(8,128)S(1)}, u32[]{:S(2)}, u32[]{:S(2)}) %collective-permute-start.4) | collective-permute-done | bytes 483360 | tf_op jit(solution)/shard_map/ppermute | solution.py:27
  57.8 0.9 %broadcast_select_fusion.1 = f32[59,2048]{1,0:T(8,128)} fusion(f32[59,2048]{1,0:T(8,128)S(1)} %collective-permute-done.4.mr, f32[59,2048]{1,0:T(8,128)S(1)} %get-tuple-element.14.mo, pred[]{:T(512)S(6)} %eq.8), kind=kLoop, calls=%fused_computation.6 | loop fusion | flops 120832 | bytes 1449985 | tf_op jit(solution)/shard_map/jit(_where)/select_n | solution.py:83
  58.8 10.3 %collective-permute-done.vr = f32[59,2048]{1,0:T(8,128)S(1)} collective-permute-done((f32[59,2048]{1,0:T(8,128)S(1)}, f32[59,2048]{1,0:T(8,128)S(1)}, u32[]{:S(2)}, u32[]{:S(2)}) %collective-permute-start) | collective-permute-done | bytes 483360 | tf_op jit(solution)/shard_map/ppermute | solution.py:27
  69.1 0.9 %broadcast_select_fusion.3 = f32[59,2048]{1,0:T(8,128)} fusion(f32[59,2048]{1,0:T(8,128)S(1)} %collective-permute-done.vr, f32[59,2048]{1,0:T(8,128)S(1)} %get-tuple-element.15.vo, pred[]{:T(512)S(6)} %eq.8), kind=kLoop, calls=%fused_computation.8 | loop fusion | flops 120832 | bytes 1449985 | tf_op jit(solution)/shard_map/jit(_where)/select_n | solution.py:83
  70.0 7.7 %collective-permute-done.2.pr = f32[59,2048]{1,0:T(8,128)S(1)} collective-permute-done((f32[59,2048]{1,0:T(8,128)S(1)}, f32[59,2048]{1,0:T(8,128)S(1)}, u32[]{:S(2)}, u32[]{:S(2)}) %collective-permute-start.2) | collective-permute-done | bytes 483360 | tf_op jit(solution)/shard_map/ppermute | solution.py:27
  77.8 0.8 copy-done.6
  78.6 0.1 reduce_max.29
  78.7 0.1 reduce_max.28
  78.8 0.1 broadcast_compare_fusion.1
  78.9 0.1 select_reduce_fusion
  79.0 0.8 convert_reduce_fusion
  79.8 0.7 collective-permute-done.3.ps
  80.5 0.8 copy-done.8
  81.3 4.0 %compact.1 = (f32[59,2048]{1,0:T(8,128)}, f32[59,2048]{1,0:T(8,128)}, f32[59,2048]{1,0:T(8,128)}) custom-call(s32[16]{0:T(128)} %get-tuple-element.11.index, s32[16]{0:T(128)} %get-tuple-element.10.valid, f32[59,2048]{1,0:T(8,128)} %copy-done.2, f32[59,2048]{1,0:T(8,128)} %copy-done.8, f32[59,2048]{1,0:T(8,128)} %copy-done.6, f32[59,2048]{1,0:T(8,128)} %copy-done.1, ...), custom_call_target="tpu_custom_call" | custom-call | tf_op jit(solution)/shard_map/compact/pallas_call | solution.py:109
  (32 shorter events, 0.2 us)
Async XLA Ops:
  0.6 34.7 %copy-start.4 = (f32[59,2048]{1,0:T(8,128)S(1)}, f32[59,2048]{1,0:T(8,128)}, u32[]{:S(2)}) copy-start(f32[59,2048]{1,0:T(8,128)} %param.6) | copy-start | bytes 1449988
  5.3 5.3 %copy-start.9 = (s32[2048]{0:T(1024)S(1)}, s32[2048]{0:T(1024)}, u32[]{:S(2)}) copy-start(s32[2048]{0:T(1024)} %param.9) | copy-start | bytes 24580
  5.9 7.8 %all-to-all-start = ((f32[8,1,2]{2,1,0:T(1,128)}), f32[8,1,2]{2,1,0:T(1,128)S(1)}, u32[]{:S(2)}, u32[]{:S(2)}) async-start(f32[8,1,2]{2,1,0:T(1,128)} %broadcast_in_dim.73), calls=%async_computation | async-start | bytes 8192 | tf_op jit(solution)/shard_map/all_to_all | solution.py:36
  14.4 19.5 %all-to-all-start.1 = ((f32[32,1,2]{2,1,0:T(1,128)}), f32[32,1,2]{2,1,0:T(1,128)S(1)}, u32[]{:S(2)}, u32[]{:S(2)}) async-start(f32[32,1,2]{2,1,0:T(1,128)} %broadcast_in_dim.74), calls=%async_computation.1 | async-start | bytes 32768 | tf_op jit(solution)/shard_map/all_to_all | solution.py:36
  36.9 21.9 %copy-start = (f32[59,2048]{1,0:T(8,128)}, f32[59,2048]{1,0:T(8,128)S(1)}, u32[]{:S(2)}) copy-start(f32[59,2048]{1,0:T(8,128)S(1)} %get-tuple-element.14.mo) | copy-start | bytes 1449988
  36.9 32.2 %copy-start.1 = (f32[59,2048]{1,0:T(8,128)}, f32[59,2048]{1,0:T(8,128)S(1)}, u32[]{:S(2)}) copy-start(f32[59,2048]{1,0:T(8,128)S(1)} %get-tuple-element.15.vo) | copy-start | bytes 1449988
  36.9 40.8 %copy-start.2 = (f32[59,2048]{1,0:T(8,128)}, f32[59,2048]{1,0:T(8,128)S(1)}, u32[]{:S(2)}) copy-start(f32[59,2048]{1,0:T(8,128)S(1)} %get-tuple-element.16.po) | copy-start | bytes 1449988
  36.9 20.9 %collective-permute-start.4 = (f32[59,2048]{1,0:T(8,128)S(1)}, f32[59,2048]{1,0:T(8,128)S(1)}, u32[]{:S(2)}, u32[]{:S(2)}) collective-permute-start(f32[59,2048]{1,0:T(8,128)S(1)} %get-tuple-element.14.mo), channel_id=1, source_target_pairs={{2,0},{3,1},{4,2},{5,3},{6,4},{7,5},{8,6},{9,7},{10,8},{11,9},{12,... | collective-permute-start | bytes 1449992 | tf_op jit(solution)/shard_map/ppermute | solution.py:27
  42.0 27.1 %collective-permute-start = (f32[59,2048]{1,0:T(8,128)S(1)}, f32[59,2048]{1,0:T(8,128)S(1)}, u32[]{:S(2)}, u32[]{:S(2)}) collective-permute-start(f32[59,2048]{1,0:T(8,128)S(1)} %get-tuple-element.15.vo), channel_id=1, source_target_pairs={{2,0},{3,1},{4,2},{5,3},{6,4},{7,5},{8,6},{9,7},{10,8},{11,9},{12,... | collective-permute-start | bytes 1449992 | tf_op jit(solution)/shard_map/ppermute | solution.py:27
  45.4 32.3 %collective-permute-start.2 = (f32[59,2048]{1,0:T(8,128)S(1)}, f32[59,2048]{1,0:T(8,128)S(1)}, u32[]{:S(2)}, u32[]{:S(2)}) collective-permute-start(f32[59,2048]{1,0:T(8,128)S(1)} %get-tuple-element.16.po), channel_id=1, source_target_pairs={{2,0},{3,1},{4,2},{5,3},{6,4},{7,5},{8,6},{9,7},{10,8},{11,9},{12,... | collective-permute-start | bytes 1449992 | tf_op jit(solution)/shard_map/ppermute | solution.py:27
  57.8 12.1 %copy-start.5 = (f32[59,2048]{1,0:T(8,128)}, f32[59,2048]{1,0:T(8,128)S(1)}, u32[]{:S(2)}) copy-start(f32[59,2048]{1,0:T(8,128)S(1)} %collective-permute-done.4.mr) | copy-start | bytes 1449988
  58.8 21.0 %collective-permute-start.5 = (f32[59,2048]{1,0:T(8,128)}, f32[59,2048]{1,0:T(8,128)}, u32[]{:S(2)}, u32[]{:S(2)}) collective-permute-start(f32[59,2048]{1,0:T(8,128)} %broadcast_select_fusion.1), channel_id=1, source_target_pairs={{0,1},{1,0},{2,3},{3,2},{4,5},{5,4},{6,7},{7,6},{8,9},{9,8},{10,11... | collective-permute-start | bytes 1449992 | tf_op jit(solution)/shard_map/ppermute | solution.py:31
  69.1 9.5 %copy-start.3 = (f32[59,2048]{1,0:T(8,128)}, f32[59,2048]{1,0:T(8,128)S(1)}, u32[]{:S(2)}) copy-start(f32[59,2048]{1,0:T(8,128)S(1)} %collective-permute-done.vr) | copy-start | bytes 1449988
  70.0 8.7 %collective-permute-start.1 = (f32[59,2048]{1,0:T(8,128)}, f32[59,2048]{1,0:T(8,128)S(1)}, u32[]{:S(2)}, u32[]{:S(2)}) collective-permute-start(f32[59,2048]{1,0:T(8,128)} %broadcast_select_fusion.3), channel_id=1, source_target_pairs={{0,1},{1,0},{2,3},{3,2},{4,5},{5,4},{6,7},{7,6},{8,9},{9,8},{10,11... | collective-permute-start | bytes 1449992 | tf_op jit(solution)/shard_map/ppermute | solution.py:31
  77.7 0.8 copy-start.6
  78.6 1.9 %collective-permute-start.3 = (f32[59,2048]{1,0:T(8,128)S(1)}, f32[59,2048]{1,0:T(8,128)S(1)}, u32[]{:S(2)}, u32[]{:S(2)}) collective-permute-start(f32[59,2048]{1,0:T(8,128)S(1)} %broadcast_select_fusion.2), channel_id=1, source_target_pairs={{0,1},{1,0},{2,3},{3,2},{4,5},{5,4},{6,7},{7,6},{8,9},{9,8},{10,11... | collective-permute-start | bytes 1449992 | tf_op jit(solution)/shard_map/ppermute | solution.py:31
  78.7 1.8 %copy-start.7 = (f32[59,2048]{1,0:T(8,128)}, f32[59,2048]{1,0:T(8,128)S(1)}, u32[]{:S(2)}) copy-start(f32[59,2048]{1,0:T(8,128)S(1)} %collective-permute-done.1.vs) | copy-start | bytes 1449988
  80.5 0.8 copy-start.8

commit v2 on v1

v2 whole, which is shorter than its diff:
```python
import jax
import jax.numpy as jnp
from jax import lax
from jax.experimental import pallas as pl
from jax.experimental.pallas import tpu as pltpu
from jax.sharding import Mesh
from jax.sharding import PartitionSpec as P


FEATURES = 59
BLOCK = 128
BLOCKS = 16
STEP = 10
DEVICES = 256
AXES = ("gx", "gy", "gz_0", "gz_1")
NEAR = ("gz_0", "gz_1")
FAR = ("gx", "gy")
CHUNKS = ((0, 24), (24, 24), (48, 11))

beta_one = 0.9
beta_two = 0.999
learn_rate = 0.05
adam_eps = 1e-08
clip_rms = 1.0
correct_one = 1.0 - beta_one**STEP
correct_two = 1.0 - beta_two**STEP

ANY = pl.BlockSpec(memory_space=pl.ANY)
SMEM = pl.BlockSpec(memory_space=pltpu.SMEM)
VMEM = pl.BlockSpec(memory_space=pltpu.VMEM)


def pack_kernel(p_ref, g_ref, m_ref, v_ref, mask_ref, pair_ref, *chunks):
    grads = g_ref[...]
    square = jnp.sum(grads * grads)
    alive = (jnp.max(mask_ref[...], axis=1, keepdims=True) > 0).astype(jnp.float32)
    lane = lax.broadcasted_iota(jnp.int32, (BLOCKS, BLOCK), 1)
    block = lax.broadcasted_iota(jnp.int32, (BLOCKS, BLOCK), 0)
    chosen = (lane == block + 2) | (lane == 1)
    row = jnp.sum(jnp.where(chosen, alive, 0.0), axis=0, keepdims=True)
    first_lane = lax.broadcasted_iota(jnp.int32, (1, BLOCK), 1)
    row = jnp.where(first_lane == 0, square, row)
    pair_ref[...] = jnp.broadcast_to(row[None], pair_ref.shape)
    for (start, count), out in zip(CHUNKS, chunks):
        rows = slice(start, start + count)
        out[0:count, :] = p_ref[rows, :]
        out[count : 2 * count, :] = g_ref[rows, :]
        out[2 * count : 3 * count, :] = m_ref[rows, :]
    for b in range(BLOCKS):
        here = slice(b * BLOCK, (b + 1) * BLOCK)
        kept = mask_ref[b : b + 1, :] > 0
        for (start, count), out in zip(CHUNKS, chunks):
            value = v_ref[start : start + count, here]
            out[3 * count : 4 * count, here] = jnp.where(kept, value, 0.0)


def line_kernel(near_ref, far_ref):
    near = near_ref[:, 0, :]
    lane = lax.broadcasted_iota(jnp.int32, (1, BLOCK), 1)
    total = jnp.sum(near, axis=0, keepdims=True)
    second = pltpu.roll(near[1:2], BLOCKS, 1)
    row = jnp.where(lane < 2 + BLOCKS, near[0:1], second)
    row = jnp.where(lane < 2, total, jnp.where(lane < 2 + 2 * BLOCKS, row, 0.0))
    far_ref[...] = jnp.broadcast_to(row[None], far_ref.shape)


def table_kernel(near_ref, far_ref, place_ref, scale_ref):
    y_core = lax.axis_index("gz_0") * 2 + lax.axis_index("gz_1")
    line = lax.axis_index("gx") * 4 + lax.axis_index("gy")
    near = near_ref[:, 0, :]
    far = far_ref[:, 0, :]
    near_row = lax.broadcasted_iota(jnp.int32, near.shape, 0)
    far_row = lax.broadcasted_iota(jnp.int32, far.shape, 0)
    lane = lax.broadcasted_iota(jnp.int32, (1, BLOCK), 1)

    lower = jnp.sum(jnp.where(near_row < y_core, near, 0.0), axis=0, keepdims=True)
    lower += jnp.sum(jnp.where(far_row < line, far, 0.0), axis=0, keepdims=True)
    lower = jnp.sum(jnp.where(lane == 1, lower, 0.0), axis=1, keepdims=True)
    total = jnp.sum(far, axis=0, keepdims=True)
    total = jnp.sum(jnp.where(lane == 0, total, 0.0), axis=1, keepdims=True)
    rms = jnp.sqrt(total / (FEATURES * BLOCKS * BLOCK * DEVICES))
    clip = jnp.minimum(1.0, clip_rms / (rms + 1e-06))
    scale_ref[...] = jnp.where(lane == 0, clip, rms)

    def near_flags(device):
        return jnp.sum(jnp.where(near_row == device, near, 0.0), axis=0, keepdims=True)

    after = jnp.sum(jnp.where(far_row == line + 1, far, 0.0), axis=0, keepdims=True)
    later = pltpu.roll(after, BLOCK - BLOCKS, 1)
    own = near_flags(y_core)
    middle = jnp.where(y_core < 7, near_flags(y_core + 1), after)
    last = jnp.where(y_core < 6, near_flags(y_core + 2), jnp.where(y_core == 6, after, later))
    flags = jnp.where(
        lane < BLOCKS,
        pltpu.roll(own, BLOCK - 2, 1),
        jnp.where(
            lane < 2 * BLOCKS, pltpu.roll(middle, BLOCKS - 2, 1), pltpu.roll(last, 2 * BLOCKS - 2, 1)
        ),
    )
    window = (3 * BLOCKS, BLOCK)
    flags = jnp.broadcast_to(flags, window)
    row = lax.broadcasted_iota(jnp.int32, window, 0)
    column = lax.broadcasted_iota(jnp.int32, window, 1)
    rank = jnp.sum(jnp.where(column < row, flags, 0.0), axis=1, keepdims=True)
    alive = jnp.sum(jnp.where(column == row, flags, 0.0), axis=1, keepdims=True)
    device = line * 8 + y_core
    wanted = (device * BLOCKS).astype(jnp.float32) - lower + column.astype(jnp.float32)
    match = (rank == wanted) & (alive > 0.0)
    place = jnp.sum(jnp.where(match, row + 1, 0), axis=0, keepdims=True)
    place_ref[...] = place


def update_kernel(start, count, place, scale, own, below, above, received, *refs):
    p_all, m_all, v_all, block, p_rows, m_rows, v_rows, sems, out_sems = refs[-9:]
    core = lax.axis_index("gz_1")

    def landing(slot):
        return block.at[:, pl.ds(slot * BLOCK, BLOCK)]

    for slot in range(BLOCKS):
        at = jnp.maximum(place[0, slot] - 1, 0)
        part = at // BLOCKS
        lanes = pl.ds(pl.multiple_of((at % BLOCKS) * BLOCK, BLOCK), BLOCK)
        cases = (
            (part == 0, own),
            ((part == 1) & (core == 0), below),
            ((part == 1) & (core == 1), above),
            (part == 2, received),
        )
        for condition, ref in cases:

            @pl.when(condition)
            def _(ref=ref, lanes=lanes, slot=slot):
                pltpu.make_async_copy(ref.at[:, lanes], landing(slot), sems.at[slot]).start()

    factor = scale[0, 0]
    for slot in range(BLOCKS):
        here = pl.ds(slot * BLOCK, BLOCK)
        pltpu.make_async_copy(own.at[:, pl.ds(0, BLOCK)], landing(slot), sems.at[slot]).wait()
        second = block[3 * count : 4 * count, here]
        kept = (second > 0.0) & (place[0, slot] > 0)
        clipped = factor * block[count : 2 * count, here]
        first = beta_one * block[2 * count : 3 * count, here] + (1.0 - beta_one) * clipped
        second = beta_two * second + (1.0 - beta_two) * clipped * clipped
        updated = block[0:count, here] - learn_rate * (first / correct_one) / (
            jnp.sqrt(second / correct_two) + adam_eps
        )
        p_rows[:, here] = jnp.where(kept, updated, 0.0)
        m_rows[:, here] = jnp.where(kept, first, 0.0)
        v_rows[:, here] = jnp.where(kept, second, 0.0)
    rows = pl.ds(start, count)
    copies = [
        pltpu.make_async_copy(rows_ref, whole.at[rows, :], out_sems.at[i])
        for i, (rows_ref, whole) in enumerate(((p_rows, p_all), (m_rows, m_all), (v_rows, v_all)))
    ]
    for copy in copies:
        copy.start()
    for copy in copies:
        copy.wait()


def update_rows(start, count, place, scale, parts, outs, out_type):
    operands = (place, scale, *parts, *outs)
    return pl.pallas_call(
        lambda *refs: update_kernel(start, count, *refs),
        out_shape=(out_type,) * 3,
        in_specs=[SMEM, SMEM] + [ANY] * (len(operands) - 2),
        out_specs=(ANY,) * 3,
        input_output_aliases={6 + i: i for i in range(len(outs))},
        scratch_shapes=[
            pltpu.VMEM((4 * count, BLOCKS * BLOCK), jnp.float32),
            *[pltpu.VMEM((count, BLOCKS * BLOCK), jnp.float32)] * 3,
            pltpu.SemaphoreType.DMA((BLOCKS,)),
            pltpu.SemaphoreType.DMA((3,)),
        ],
        cost_estimate=pl.CostEstimate(flops=10000000, bytes_accessed=2000000, transcendentals=0),
        name="update",
    )(*operands)


def shards(params, gradients, moment_one, moment_two, keep_mask):
    row_count = params.shape[1]
    f32 = jnp.float32
    pairs, *own = pl.pallas_call(
        pack_kernel,
        out_shape=(
            jax.ShapeDtypeStruct((8, 1, BLOCK), f32),
            *[jax.ShapeDtypeStruct((4 * count, row_count), f32) for _, count in CHUNKS],
        ),
        in_specs=[VMEM] * 5,
        out_specs=(VMEM,) * (1 + len(CHUNKS)),
        name="pack",
    )(params, gradients, moment_one, moment_two, keep_mask.reshape(BLOCKS, BLOCK))

    near = lax.all_to_all(pairs, NEAR, 0, 0, tiled=True)
    lines = pl.pallas_call(
        line_kernel,
        out_shape=jax.ShapeDtypeStruct((32, 1, BLOCK), f32),
        name="line",
    )(near)
    far = lax.all_to_all(lines, FAR, 0, 0, tiled=True)
    place, scale = pl.pallas_call(
        table_kernel,
        out_shape=(
            jax.ShapeDtypeStruct((1, BLOCK), jnp.int32),
            jax.ShapeDtypeStruct((1, BLOCK), f32),
        ),
        name="table",
    )(near, far)

    out_type = jax.ShapeDtypeStruct(params.shape, f32)
    outs = ()
    for i, (start, count) in enumerate(CHUNKS):
        received = lax.ppermute(own[i], AXES, [(d, d - 2) for d in range(2, DEVICES)])
        below = lax.ppermute(own[i], "gz_1", [(1, 0)])
        above = lax.ppermute(received, "gz_1", [(0, 1)])
        parts = (own[i], below, above, received)
        outs = update_rows(start, count, place, scale, parts, outs, out_type)
    return (*outs, scale[0, 1])


def solution(mesh):
    split = Mesh(mesh.devices.reshape(mesh.shape["gx"], mesh.shape["gy"], 4, 2), AXES)
    spec = P(None, AXES)

    return jax.shard_map(
        shards,
        mesh=split,
        in_specs=(spec, spec, spec, spec, P(AXES)),
        out_specs=(spec, spec, spec, P()),
        check_vma=False,
    )
```

time: 87.1 us -> 114 us (1.31)
  the two profiles are of different devices: /device:TPU:30 before, /device:TPU:1 now
where the time goes in v2:
time: 114 us; the launch traced here: 113 us
  blocking collectives  38.7 us (34%)
  waiting for transfers between devices  28.8 us (25%)
  starting transfers between devices  28.2 us (25%)
  Pallas kernels  14.6 us (13%)
  local copies, waits for them, and re-layouts  2.39 us (2%)
    ppermute x3, waiting for transfers between devices, shards(): lax.ppermute(own[i], AXES, [(d, d - 2) for d in range(2, DEVICES)])  28.8 us
    all_to_all x1, blocking collectives, shards(): far = lax.all_to_all(lines, FAR, 0, 0, tiled=True)  23.6 us
    ppermute x3, starting transfers between devices, shards(): below = lax.ppermute(own[i], 'gz_1', [(1, 0)])  20.3 us
    all_to_all x1, blocking collectives, shards(): near = lax.all_to_all(pairs, NEAR, 0, 0, tiled=True)  15 us
    pallas_call x3, Pallas kernels, update_rows(): pl.pallas_call(lambda *refs: update_kernel(start, count, *refs), out_shap...  8.69 us
    ppermute x3, starting transfers between devices, shards(): lax.ppermute(own[i], AXES, [(d, d - 2) for d in range(2, DEVICES)])  4 us
    ppermute x3, starting transfers between devices, shards(): above = lax.ppermute(received, 'gz_1', [(0, 1)])  3.84 us
    pallas_call x1, Pallas kernels, shards(): pl.pallas_call(pack_kernel, out_shape=(jax.ShapeDtypeStruct((8, 1, BLOCK)...  3 us
  transfers between devices with their start and end apart: 9, of which 3 were waited for; matrix products, arithmetic and copies ran while one was open for 1% of the time, Pallas kernels for 8%

profile of v2, /device:TPU:1, one launch (start us, length us, event | category | flops | bytes accessed | tf_op | source)
XLA Modules:
  0.0 113.5 jit_solution(3352889253349744354)
XLA Ops:
  0.6 3.0 %pack.1 = (f32[8,1,128]{2,1,0:T(1,128)}, f32[96,2048]{1,0:T(8,128)}, f32[96,2048]{1,0:T(8,128)}, f32[44,2048]{1,0:T(8,128)}) custom-call(f32[59,2048]{1,0:T(8,128)} %p_ref.1, f32[59,2048]{1,0:T(8,128)} %g_ref.1, f32[59,2048]{1,0:T(8,128)} %m_ref.1, f32[59,2048]{1,0:T(8,128)} %v_ref.1, s32[16,128]{1,0:T(8,128)} %bitcast.2), custom_call_target="tpu_custom_call" | custom-call | tf_op jit(solution)/shard_map/pack/pallas_call | solution.py:184
  3.6 1.4 %collective-permute-start.7 = (f32[96,2048]{1,0:T(8,128)}, f32[96,2048]{1,0:T(8,128)S(1)}, u32[]{:S(2)}, u32[]{:S(2)}) collective-permute-start(f32[96,2048]{1,0:T(8,128)} %get-tuple-element.24.refs_2_), channel_id=1, source_target_pairs={{2,0},{3,1},{4,2},{5,3},{6,4},{7,5},{8,6},{9,7},{10,8},{11,9},{12,... | collective-permute-start | bytes 2359304 | tf_op jit(solution)/shard_map/ppermute | solution.py:214
  5.1 1.3 %collective-permute-start.4 = (f32[96,2048]{1,0:T(8,128)}, f32[96,2048]{1,0:T(8,128)S(1)}, u32[]{:S(2)}, u32[]{:S(2)}) collective-permute-start(f32[96,2048]{1,0:T(8,128)} %get-tuple-element.23.refs_2_), channel_id=1, source_target_pairs={{2,0},{3,1},{4,2},{5,3},{6,4},{7,5},{8,6},{9,7},{10,8},{11,9},{12,... | collective-permute-start | bytes 2359304 | tf_op jit(solution)/shard_map/ppermute | solution.py:214
  6.4 6.0 %collective-permute-start.6 = (f32[96,2048]{1,0:T(8,128)}, f32[96,2048]{1,0:T(8,128)}, u32[]{:S(2)}, u32[]{:S(2)}) collective-permute-start(f32[96,2048]{1,0:T(8,128)} %get-tuple-element.24.refs_2_), channel_id=1, source_target_pairs={{1,0},{3,2},{5,4},{7,6},{9,8},{11,10},{13,12},{15,14},{17,16},{19,... | collective-permute-start | bytes 2359304 | tf_op jit(solution)/shard_map/ppermute | solution.py:215
  12.4 10.7 %collective-permute-done.7.refs_5_ = f32[96,2048]{1,0:T(8,128)S(1)} collective-permute-done((f32[96,2048]{1,0:T(8,128)}, f32[96,2048]{1,0:T(8,128)S(1)}, u32[]{:S(2)}, u32[]{:S(2)}) %collective-permute-start.7) | collective-permute-done | bytes 786464 | tf_op jit(solution)/shard_map/ppermute | solution.py:214
  23.1 1.3 %collective-permute-start.8 = (f32[96,2048]{1,0:T(8,128)S(1)}, f32[96,2048]{1,0:T(8,128)}, u32[]{:S(2)}, u32[]{:S(2)}) collective-permute-start(f32[96,2048]{1,0:T(8,128)S(1)} %collective-permute-done.7.refs_5_), channel_id=1, source_target_pairs={{0,1},{2,3},{4,5},{6,7},{8,9},{10,11},{12,13},{14,15},{16,17},{18,... | collective-permute-start | bytes 2359304 | tf_op jit(solution)/shard_map/ppermute | solution.py:216
  24.4 9.2 %collective-permute-start.3 = (f32[96,2048]{1,0:T(8,128)}, f32[96,2048]{1,0:T(8,128)S(1)}, u32[]{:S(2)}, u32[]{:S(2)}) collective-permute-start(f32[96,2048]{1,0:T(8,128)} %get-tuple-element.23.refs_2_), channel_id=1, source_target_pairs={{1,0},{3,2},{5,4},{7,6},{9,8},{11,10},{13,12},{15,14},{17,16},{19,... | collective-permute-start | bytes 2359304 | tf_op jit(solution)/shard_map/ppermute | solution.py:215
  33.6 6.3 %collective-permute-done.4.refs_5_ = f32[96,2048]{1,0:T(8,128)S(1)} collective-permute-done((f32[96,2048]{1,0:T(8,128)}, f32[96,2048]{1,0:T(8,128)S(1)}, u32[]{:S(2)}, u32[]{:S(2)}) %collective-permute-start.4) | collective-permute-done | bytes 786464 | tf_op jit(solution)/shard_map/ppermute | solution.py:214
  39.9 1.3 %collective-permute-start.5 = (f32[96,2048]{1,0:T(8,128)S(1)}, f32[96,2048]{1,0:T(8,128)S(1)}, u32[]{:S(2)}, u32[]{:S(2)}) collective-permute-start(f32[96,2048]{1,0:T(8,128)S(1)} %collective-permute-done.4.refs_5_), channel_id=1, source_target_pairs={{0,1},{2,3},{4,5},{6,7},{8,9},{10,11},{12,13},{14,15},{16,17},{18,... | collective-permute-start | bytes 2359304 | tf_op jit(solution)/shard_map/ppermute | solution.py:216
  41.2 1.3 %collective-permute-start.1 = (f32[44,2048]{1,0:T(8,128)}, f32[44,2048]{1,0:T(8,128)S(1)}, u32[]{:S(2)}, u32[]{:S(2)}) collective-permute-start(f32[44,2048]{1,0:T(8,128)} %get-tuple-element.22.refs_2_), channel_id=1, source_target_pairs={{2,0},{3,1},{4,2},{5,3},{6,4},{7,5},{8,6},{9,7},{10,8},{11,9},{12,... | collective-permute-start | bytes 1081352 | tf_op jit(solution)/shard_map/ppermute | solution.py:214
  42.5 11.8 %collective-permute-done.1.refs_5_ = f32[44,2048]{1,0:T(8,128)S(1)} collective-permute-done((f32[44,2048]{1,0:T(8,128)}, f32[44,2048]{1,0:T(8,128)S(1)}, u32[]{:S(2)}, u32[]{:S(2)}) %collective-permute-start.1) | collective-permute-done | bytes 360480 | tf_op jit(solution)/shard_map/ppermute | solution.py:214
  54.3 5.1 %collective-permute-start = (f32[44,2048]{1,0:T(8,128)}, f32[44,2048]{1,0:T(8,128)}, u32[]{:S(2)}, u32[]{:S(2)}) collective-permute-start(f32[44,2048]{1,0:T(8,128)} %get-tuple-element.22.refs_2_), channel_id=1, source_target_pairs={{1,0},{3,2},{5,4},{7,6},{9,8},{11,10},{13,12},{15,14},{17,16},{19,... | collective-permute-start | bytes 1081352 | tf_op jit(solution)/shard_map/ppermute | solution.py:215
  59.4 0.0 collective-permute-done.6.refs_3_
  59.4 1.3 %collective-permute-start.2 = (f32[44,2048]{1,0:T(8,128)S(1)}, f32[44,2048]{1,0:T(8,128)}, u32[]{:S(2)}, u32[]{:S(2)}) collective-permute-start(f32[44,2048]{1,0:T(8,128)S(1)} %collective-permute-done.1.refs_5_), channel_id=1, source_target_pairs={{0,1},{2,3},{4,5},{6,7},{8,9},{10,11},{12,13},{14,15},{16,17},{18,... | collective-permute-start | bytes 1081352 | tf_op jit(solution)/shard_map/ppermute | solution.py:216
  60.7 0.0 copy-done.6
  60.7 15.0 %all_to_all.10.near_ref = f32[8,1,128]{2,1,0:T(1,128)} all-to-all(f32[8,1,128]{2,1,0:T(1,128)S(1)} %copy-done.6), channel_id=1, replica_groups=mesh['gx'=8,'gy'=4,'gz_0'=4,'gz_1'=2] {'gz_0','gz_1'}, dimensions={0} | all-to-all | bytes 8192 | tf_op jit(solution)/shard_map/all_to_all | solution.py:195
  75.7 1.4 %line.1 = f32[32,1,128]{2,1,0:T(1,128)} custom-call(f32[8,1,128]{2,1,0:T(1,128)} %all_to_all.10.near_ref), custom_call_target="tpu_custom_call" | custom-call | tf_op jit(solution)/shard_map/line/pallas_call | solution.py:196
  77.1 23.6 %all_to_all.11.far_ref = f32[32,1,128]{2,1,0:T(1,128)} all-to-all(f32[32,1,128]{2,1,0:T(1,128)} %line.1), channel_id=1, replica_groups=mesh['gx'=8,'gy'=4,'gz_0'=4,'gz_1'=2] {'gx','gy'}, dimensions={0} | all-to-all | bytes 32768 | tf_op jit(solution)/shard_map/all_to_all | solution.py:201
  100.7 1.6 %table.1 = (s32[1,128]{1,0:T(1,128)}, f32[1,128]{1,0:T(1,128)}) custom-call(f32[8,1,128]{2,1,0:T(1,128)} %all_to_all.10.near_ref, f32[32,1,128]{2,1,0:T(1,128)} %all_to_all.11.far_ref), custom_call_target="tpu_custom_call" | custom-call | tf_op jit(solution)/shard_map/table/pallas_call | solution.py:202
  102.3 0.7 copy-done.5
  103.0 0.6 slice.3
  103.6 0.0 collective-permute-done.8.refs_4_
  103.6 2.9 %update.3 = (f32[59,2048]{1,0:T(8,128)}, f32[59,2048]{1,0:T(8,128)}, f32[59,2048]{1,0:T(8,128)}) custom-call(s32[1,128]{1,0:T(1,128)} %get-tuple-element.20.refs_0_, f32[1,128]{1,0:T(1,128)} %get-tuple-element.21.refs_1_, f32[96,2048]{1,0:T(8,128)} %get-tuple-element.24.refs_2_, f32[96,2048]{1,0:T(8,128)} %collective-permute-done.6.refs_3_, ...), custom_call_target="tpu_custom_call" | custom-call | flops 10000000 | bytes 2000000 | tf_op jit(solution)/shard_map/update/pallas_call | solution.py:164
  106.5 0.0 collective-permute-done.3.refs_3_
  106.5 0.0 copy-start.1
  106.5 0.0 collective-permute-done.5.refs_4_
  106.5 0.8 copy-done.1
  107.4 0.3 copy-done.2
  107.6 2.9 %update.4 = (f32[59,2048]{1,0:T(8,128)}, f32[59,2048]{1,0:T(8,128)}, f32[59,2048]{1,0:T(8,128)}) custom-call(s32[1,128]{1,0:T(1,128)} %get-tuple-element.20.refs_0_, f32[1,128]{1,0:T(1,128)} %get-tuple-element.21.refs_1_, f32[96,2048]{1,0:T(8,128)} %get-tuple-element.23.refs_2_, ...), custom_call_target="tpu_custom_call", output_to_operand_aliasing={{0}: (6, {}), {1}: (7, {}), {2}: (8, {})} | custom-call | flops 10000000 | bytes 2000000 | tf_op jit(solution)/shard_map/update/pallas_call | solution.py:164
  110.6 0.0 collective-permute-done.refs_3_
  110.6 0.0 collective-permute-done.2.refs_4_
  110.6 2.9 %update.5 = (f32[59,2048]{1,0:T(8,128)}, f32[59,2048]{1,0:T(8,128)}, f32[59,2048]{1,0:T(8,128)}) custom-call(s32[1,128]{1,0:T(1,128)} %get-tuple-element.20.refs_0_, f32[1,128]{1,0:T(1,128)} %get-tuple-element.21.refs_1_, f32[44,2048]{1,0:T(8,128)} %get-tuple-element.22.refs_2_, ...), custom_call_target="tpu_custom_call", output_to_operand_aliasing={{0}: (6, {}), {1}: (7, {}), {2}: (8, {})} | custom-call | flops 10000000 | bytes 2000000 | tf_op jit(solution)/shard_map/update/pallas_call | solution.py:164
  (9 shorter events, 0.0 us)
Async XLA Ops:
  3.6 57.1 %copy-start.6 = (f32[8,1,128]{2,1,0:T(1,128)S(1)}, f32[8,1,128]{2,1,0:T(1,128)}, u32[]{:S(2)}) copy-start(f32[8,1,128]{2,1,0:T(1,128)} %get-tuple-element.19) | copy-start | bytes 12292
  3.6 19.4 %collective-permute-start.7 = (f32[96,2048]{1,0:T(8,128)}, f32[96,2048]{1,0:T(8,128)S(1)}, u32[]{:S(2)}, u32[]{:S(2)}) collective-permute-start(f32[96,2048]{1,0:T(8,128)} %get-tuple-element.24.refs_2_), channel_id=1, source_target_pairs={{2,0},{3,1},{4,2},{5,3},{6,4},{7,5},{8,6},{9,7},{10,8},{11,9},{12,... | collective-permute-start | bytes 2359304 | tf_op jit(solution)/shard_map/ppermute | solution.py:214
  5.1 34.9 %collective-permute-start.4 = (f32[96,2048]{1,0:T(8,128)}, f32[96,2048]{1,0:T(8,128)S(1)}, u32[]{:S(2)}, u32[]{:S(2)}) collective-permute-start(f32[96,2048]{1,0:T(8,128)} %get-tuple-element.23.refs_2_), channel_id=1, source_target_pairs={{2,0},{3,1},{4,2},{5,3},{6,4},{7,5},{8,6},{9,7},{10,8},{11,9},{12,... | collective-permute-start | bytes 2359304 | tf_op jit(solution)/shard_map/ppermute | solution.py:214
  6.4 53.0 %collective-permute-start.6 = (f32[96,2048]{1,0:T(8,128)}, f32[96,2048]{1,0:T(8,128)}, u32[]{:S(2)}, u32[]{:S(2)}) collective-permute-start(f32[96,2048]{1,0:T(8,128)} %get-tuple-element.24.refs_2_), channel_id=1, source_target_pairs={{1,0},{3,2},{5,4},{7,6},{9,8},{11,10},{13,12},{15,14},{17,16},{19,... | collective-permute-start | bytes 2359304 | tf_op jit(solution)/shard_map/ppermute | solution.py:215
  23.1 80.5 %copy-start.3 = (f32[96,2048]{1,0:T(8,128)}, f32[96,2048]{1,0:T(8,128)S(1)}, u32[]{:S(2)}) copy-start(f32[96,2048]{1,0:T(8,128)S(1)} %collective-permute-done.7.refs_5_) | copy-start | bytes 2359300
  23.1 80.5 %collective-permute-start.8 = (f32[96,2048]{1,0:T(8,128)S(1)}, f32[96,2048]{1,0:T(8,128)}, u32[]{:S(2)}, u32[]{:S(2)}) collective-permute-start(f32[96,2048]{1,0:T(8,128)S(1)} %collective-permute-done.7.refs_5_), channel_id=1, source_target_pairs={{0,1},{2,3},{4,5},{6,7},{8,9},{10,11},{12,13},{14,15},{16,17},{18,... | collective-permute-start | bytes 2359304 | tf_op jit(solution)/shard_map/ppermute | solution.py:216
  24.4 82.1 %collective-permute-start.3 = (f32[96,2048]{1,0:T(8,128)}, f32[96,2048]{1,0:T(8,128)S(1)}, u32[]{:S(2)}, u32[]{:S(2)}) collective-permute-start(f32[96,2048]{1,0:T(8,128)} %get-tuple-element.23.refs_2_), channel_id=1, source_target_pairs={{1,0},{3,2},{5,4},{7,6},{9,8},{11,10},{13,12},{15,14},{17,16},{19,... | collective-permute-start | bytes 2359304 | tf_op jit(solution)/shard_map/ppermute | solution.py:215
  39.9 66.5 %copy-start = (f32[96,2048]{1,0:T(8,128)}, f32[96,2048]{1,0:T(8,128)S(1)}, u32[]{:S(2)}) copy-start(f32[96,2048]{1,0:T(8,128)S(1)} %collective-permute-done.4.refs_5_) | copy-start | bytes 2359300
  39.9 66.6 %collective-permute-start.5 = (f32[96,2048]{1,0:T(8,128)S(1)}, f32[96,2048]{1,0:T(8,128)S(1)}, u32[]{:S(2)}, u32[]{:S(2)}) collective-permute-start(f32[96,2048]{1,0:T(8,128)S(1)} %collective-permute-done.4.refs_5_), channel_id=1, source_target_pairs={{0,1},{2,3},{4,5},{6,7},{8,9},{10,11},{12,13},{14,15},{16,17},{18,... | collective-permute-start | bytes 2359304 | tf_op jit(solution)/shard_map/ppermute | solution.py:216
  41.2 13.1 %collective-permute-start.1 = (f32[44,2048]{1,0:T(8,128)}, f32[44,2048]{1,0:T(8,128)S(1)}, u32[]{:S(2)}, u32[]{:S(2)}) collective-permute-start(f32[44,2048]{1,0:T(8,128)} %get-tuple-element.22.refs_2_), channel_id=1, source_target_pairs={{2,0},{3,1},{4,2},{5,3},{6,4},{7,5},{8,6},{9,7},{10,8},{11,9},{12,... | collective-permute-start | bytes 1081352 | tf_op jit(solution)/shard_map/ppermute | solution.py:214
  54.3 52.2 %copy-start.4 = (f32[44,2048]{1,0:T(8,128)}, f32[44,2048]{1,0:T(8,128)S(1)}, u32[]{:S(2)}) copy-start(f32[44,2048]{1,0:T(8,128)S(1)} %collective-permute-done.1.refs_5_) | copy-start | bytes 1081348
  54.3 56.3 %collective-permute-start = (f32[44,2048]{1,0:T(8,128)}, f32[44,2048]{1,0:T(8,128)}, u32[]{:S(2)}, u32[]{:S(2)}) collective-permute-start(f32[44,2048]{1,0:T(8,128)} %get-tuple-element.22.refs_2_), channel_id=1, source_target_pairs={{1,0},{3,2},{5,4},{7,6},{9,8},{11,10},{13,12},{15,14},{17,16},{19,... | collective-permute-start | bytes 1081352 | tf_op jit(solution)/shard_map/ppermute | solution.py:215
  59.4 51.2 %collective-permute-start.2 = (f32[44,2048]{1,0:T(8,128)S(1)}, f32[44,2048]{1,0:T(8,128)}, u32[]{:S(2)}, u32[]{:S(2)}) collective-permute-start(f32[44,2048]{1,0:T(8,128)S(1)} %collective-permute-done.1.refs_5_), channel_id=1, source_target_pairs={{0,1},{2,3},{4,5},{6,7},{8,9},{10,11},{12,13},{14,15},{16,17},{18,... | collective-permute-start | bytes 1081352 | tf_op jit(solution)/shard_map/ppermute | solution.py:216
  102.3 0.7 copy-start.5
  106.5 0.9 copy-start.1
  106.5 1.1 copy-start.2

commit v3 on v2

--- a/solution.py
+++ b/solution.py
@@ -15,7 +15,7 @@
 AXES = ("gx", "gy", "gz_0", "gz_1")
 NEAR = ("gz_0", "gz_1")
 FAR = ("gx", "gy")
-CHUNKS = ((0, 24), (24, 24), (48, 11))
+CHUNKS = ((24, 35), (0, 24))
 
 beta_one = 0.9
 beta_two = 0.999
@@ -30,7 +30,7 @@
 VMEM = pl.BlockSpec(memory_space=pltpu.VMEM)
 
 
-def pack_kernel(p_ref, g_ref, m_ref, v_ref, mask_ref, pair_ref, *chunks):
+def pack_kernel(g_ref, m_ref, v_ref, mask_ref, pair_ref, *chunks):
     grads = g_ref[...]
     square = jnp.sum(grads * grads)
     alive = (jnp.max(mask_ref[...], axis=1, keepdims=True) > 0).astype(jnp.float32)
@@ -43,15 +43,14 @@
     pair_ref[...] = jnp.broadcast_to(row[None], pair_ref.shape)
     for (start, count), out in zip(CHUNKS, chunks):
         rows = slice(start, start + count)
-        out[0:count, :] = p_ref[rows, :]
-        out[count : 2 * count, :] = g_ref[rows, :]
-        out[2 * count : 3 * count, :] = m_ref[rows, :]
+        out[0:count, :] = g_ref[rows, :]
+        out[count : 2 * count, :] = m_ref[rows, :]
     for b in range(BLOCKS):
         here = slice(b * BLOCK, (b + 1) * BLOCK)
         kept = mask_ref[b : b + 1, :] > 0
         for (start, count), out in zip(CHUNKS, chunks):
             value = v_ref[start : start + count, here]
-            out[3 * count : 4 * count, here] = jnp.where(kept, value, 0.0)
+            out[2 * count : 3 * count, here] = jnp.where(kept, value, 0.0)
 
 
 def line_kernel(near_ref, far_ref):
@@ -64,7 +63,7 @@
     far_ref[...] = jnp.broadcast_to(row[None], far_ref.shape)
 
 
-def table_kernel(near_ref, far_ref, place_ref, scale_ref):
+def table_kernel(near_ref, far_ref, place_ref, clip_ref, rms_ref):
     y_core = lax.axis_index("gz_0") * 2 + lax.axis_index("gz_1")
     line = lax.axis_index("gx") * 4 + lax.axis_index("gy")
     near = near_ref[:, 0, :]
@@ -80,7 +79,8 @@
     total = jnp.sum(jnp.where(lane == 0, total, 0.0), axis=1, keepdims=True)
     rms = jnp.sqrt(total / (FEATURES * BLOCKS * BLOCK * DEVICES))
     clip = jnp.minimum(1.0, clip_rms / (rms + 1e-06))
-    scale_ref[...] = jnp.where(lane == 0, clip, rms)
+    clip_ref[...] = jnp.broadcast_to(clip, clip_ref.shape)
+    rms_ref[...] = rms
 
     def near_flags(device):
         return jnp.sum(jnp.where(near_row == device, near, 0.0), axis=0, keepdims=True)
@@ -110,69 +110,74 @@
     place_ref[...] = place
 
 
-def update_kernel(start, count, place, scale, own, below, above, received, *refs):
-    p_all, m_all, v_all, block, p_rows, m_rows, v_rows, sems, out_sems = refs[-9:]
+def update_kernel(start, count, place, clip, *refs):
+    p_parts, parts = refs[0:4], refs[4:8]
+    p_all, m_all, v_all, p_block, block, p_rows, m_rows, v_rows, sems, out_sems = refs[-10:]
     core = lax.axis_index("gz_1")
-
-    def landing(slot):
-        return block.at[:, pl.ds(slot * BLOCK, BLOCK)]
+    rows = pl.ds(start, count)
+
+    def copies(p_ref, ref, lanes, slot):
+        here = pl.ds(slot * BLOCK, BLOCK)
+        return (
+            pltpu.make_async_copy(ref.at[:, lanes], block.at[:, here], sems.at[0, slot]),
+            pltpu.make_async_copy(p_ref.at[rows, lanes], p_block.at[:, here], sems.at[1, slot]),
+        )
 
     for slot in range(BLOCKS):
         at = jnp.maximum(place[0, slot] - 1, 0)
         part = at // BLOCKS
         lanes = pl.ds(pl.multiple_of((at % BLOCKS) * BLOCK, BLOCK), BLOCK)
-        cases = (
-            (part == 0, own),
-            ((part == 1) & (core == 0), below),
-            ((part == 1) & (core == 1), above),
-            (part == 2, received),
-        )
-        for condition, ref in cases:
+        cases = (part == 0, (part == 1) & (core == 0), (part == 1) & (core == 1), part == 2)
+        for condition, p_ref, ref in zip(cases, p_parts, parts):
 
             @pl.when(condition)
-            def _(ref=ref, lanes=lanes, slot=slot):
-                pltpu.make_async_copy(ref.at[:, lanes], landing(slot), sems.at[slot]).start()
-
-    factor = scale[0, 0]
+            def _(p_ref=p_ref, ref=ref, lanes=lanes, slot=slot):
+                for copy in copies(p_ref, ref, lanes, slot):
+                    copy.start()
+
+    factor = clip[0, 0]
     for slot in range(BLOCKS):
         here = pl.ds(slot * BLOCK, BLOCK)
-        pltpu.make_async_copy(own.at[:, pl.ds(0, BLOCK)], landing(slot), sems.at[slot]).wait()
-        second = block[3 * count : 4 * count, here]
+        for copy in copies(p_parts[0], parts[0], pl.ds(0, BLOCK), slot):
+            copy.wait()
+        second = block[2 * count : 3 * count, here]
         kept = (second > 0.0) & (place[0, slot] > 0)
-        clipped = factor * block[count : 2 * count, here]
-        first = beta_one * block[2 * count : 3 * count, here] + (1.0 - beta_one) * clipped
+        clipped = factor * block[0:count, here]
+        first = beta_one * block[count : 2 * count, here] + (1.0 - beta_one) * clipped
         second = beta_two * second + (1.0 - beta_two) * clipped * clipped
-        updated = block[0:count, here] - learn_rate * (first / correct_one) / (
+        updated = p_block[:, here] - learn_rate * (first / correct_one) / (
             jnp.sqrt(second / correct_two) + adam_eps
         )
         p_rows[:, here] = jnp.where(kept, updated, 0.0)
         m_rows[:, here] = jnp.where(kept, first, 0.0)
         v_rows[:, here] = jnp.where(kept, second, 0.0)
-    rows = pl.ds(start, count)
-    copies = [
+    done = [
         pltpu.make_async_copy(rows_ref, whole.at[rows, :], out_sems.at[i])
         for i, (rows_ref, whole) in enumerate(((p_rows, p_all), (m_rows, m_all), (v_rows, v_all)))
     ]
-    for copy in copies:
+    for copy in done:
         copy.start()
-    for copy in copies:
+    for copy in done:
         copy.wait()
 
 
-def update_rows(start, count, place, scale, parts, outs, out_type):
-    operands = (place, scale, *parts, *outs)
+def update_rows(start, count, place, clip, p_parts, parts, outs, out_type):
+    operands = (place, clip, *p_parts, *parts, *outs)
+    width = BLOCKS * BLOCK
     return pl.pallas_call(
         lambda *refs: update_kernel(start, count, *refs),
         out_shape=(out_type,) * 3,
         in_specs=[SMEM, SMEM] + [ANY] * (len(operands) - 2),
         out_specs=(ANY,) * 3,
-        input_output_aliases={6 + i: i for i in range(len(outs))},
+        input_output_aliases={10 + i: i for i in range(len(outs))},
         scratch_shapes=[
-            pltpu.VMEM((4 * count, BLOCKS * BLOCK), jnp.float32),
-            *[pltpu.VMEM((count, BLOCKS * BLOCK), jnp.float32)] * 3,
-            pltpu.SemaphoreType.DMA((BLOCKS,)),
+            pltpu.VMEM((count, width), jnp.float32),
+            pltpu.VMEM((3 * count, width), jnp.float32),
+            *[pltpu.VMEM((count, width), jnp.float32)] * 3,
+            pltpu.SemaphoreType.DMA((2, BLOCKS)),
             pltpu.SemaphoreType.DMA((3,)),
         ],
+        compiler_params=pltpu.CompilerParams(vmem_limit_bytes=8 * 1024 * 1024),
         cost_estimate=pl.CostEstimate(flops=10000000, bytes_accessed=2000000, transcendentals=0),
         name="update",
     )(*operands)
@@ -181,42 +186,51 @@
 def shards(params, gradients, moment_one, moment_two, keep_mask):
     row_count = params.shape[1]
     f32 = jnp.float32
+    small = pltpu.CompilerParams(vmem_limit_bytes=1024 * 1024)
+
+    def moved(x):
+        received = lax.ppermute(x, AXES, [(d, d - 2) for d in range(2, DEVICES)])
+        below = lax.ppermute(x, "gz_1", [(1, 0)])
+        above = lax.ppermute(received, "gz_1", [(0, 1)])
+        return x, below, above, received
+
     pairs, *own = pl.pallas_call(
         pack_kernel,
         out_shape=(
             jax.ShapeDtypeStruct((8, 1, BLOCK), f32),
-            *[jax.ShapeDtypeStruct((4 * count, row_count), f32) for _, count in CHUNKS],
+            *[jax.ShapeDtypeStruct((3 * count, row_count), f32) for _, count in CHUNKS],
         ),
-        in_specs=[VMEM] * 5,
+        in_specs=[VMEM] * 4,
         out_specs=(VMEM,) * (1 + len(CHUNKS)),
         name="pack",
-    )(params, gradients, moment_one, moment_two, keep_mask.reshape(BLOCKS, BLOCK))
+    )(gradients, moment_one, moment_two, keep_mask.reshape(BLOCKS, BLOCK))
 
     near = lax.all_to_all(pairs, NEAR, 0, 0, tiled=True)
     lines = pl.pallas_call(
         line_kernel,
         out_shape=jax.ShapeDtypeStruct((32, 1, BLOCK), f32),
+        compiler_params=small,
         name="line",
     )(near)
     far = lax.all_to_all(lines, FAR, 0, 0, tiled=True)
-    place, scale = pl.pallas_call(
+    place, clip, rms = pl.pallas_call(
         table_kernel,
         out_shape=(
             jax.ShapeDtypeStruct((1, BLOCK), jnp.int32),
             jax.ShapeDtypeStruct((1, BLOCK), f32),
+            jax.ShapeDtypeStruct((1, 1), f32),
         ),
+        compiler_params=small,
         name="table",
     )(near, far)
 
     out_type = jax.ShapeDtypeStruct(params.shape, f32)
+    p_parts = moved(params)
     outs = ()
     for i, (start, count) in enumerate(CHUNKS):
-        received = lax.ppermute(own[i], AXES, [(d, d - 2) for d in range(2, DEVICES)])
-        below = lax.ppermute(own[i], "gz_1", [(1, 0)])
-        above = lax.ppermute(received, "gz_1", [(0, 1)])
-        parts = (own[i], below, above, received)
-        outs = update_rows(start, count, place, scale, parts, outs, out_type)
-    return (*outs, scale[0, 1])
+        parts = moved(own[i])
+        outs = update_rows(start, count, place, clip, p_parts, parts, outs, out_type)
+    return (*outs, rms.reshape(()))
 
 
 def solution(mesh):

time: 114 us -> 99.3 us (0.87)
  starting transfers between devices: 28.2 us -> 19.7 us
  waiting for transfers between devices: 28.8 us -> 34.3 us
  blocking collectives: 38.7 us -> 33.4 us
  Pallas kernels: 14.6 us -> 9.45 us
  local copies, waits for them, and re-layouts: 2.39 us -> 1.18 us
    ppermute x9, starting transfers between devices: 28.2 us -> 19.7 us  [the longest x3 11.8 us: moved(): below = lax.ppermute(x, 'gz_1', [(1, 0)])]
    ppermute x9, waiting for transfers between devices: 28.8 us -> 34.3 us  [the longest x3 34.3 us: moved(): received = lax.ppermute(x, AXES, [(d, d - 2) for d in range(2, DEVICES)])]
    all_to_all x1, blocking collectives: 15 us -> 12.1 us  [shards(): near = lax.all_to_all(pairs, NEAR, 0, 0, tiled=True)]
    pallas_call x3 -> x2, Pallas kernels: 8.69 us -> 5.91 us  [update_rows(): pl.pallas_call(lambda *refs: update_kernel(start, count, *refs), out_shap...]
    all_to_all x1, blocking collectives: 23.6 us -> 21.3 us  [shards(): far = lax.all_to_all(lines, FAR, 0, 0, tiled=True)]
    pallas_call x1, Pallas kernels: 1.36 us -> 0.08 us  [shards(): pl.pallas_call(line_kernel, out_shape=jax.ShapeDtypeStruct((32, 1, BLOCK)...]
  transfers between devices with their start and end apart: 9 -> 9, of which waited for: 3 -> 2; matrix products, arithmetic and copies ran while one was open for 1% -> 0% of each run, Pallas kernels for 8% -> 4%
where the time goes in v3:
time: 99.3 us; the launch traced here: 98.9 us
  waiting for transfers between devices  34.3 us (35%)
  blocking collectives  33.4 us (34%)
  starting transfers between devices  19.7 us (20%)
  Pallas kernels  9.45 us (10%)
  local copies, waits for them, and re-layouts  1.18 us (1%)
    ppermute x3, waiting for transfers between devices, moved(): received = lax.ppermute(x, AXES, [(d, d - 2) for d in range(2, DEVICES)])  34.3 us
    all_to_all x1, blocking collectives, shards(): far = lax.all_to_all(lines, FAR, 0, 0, tiled=True)  21.3 us
    all_to_all x1, blocking collectives, shards(): near = lax.all_to_all(pairs, NEAR, 0, 0, tiled=True)  12.1 us
    ppermute x3, starting transfers between devices, moved(): below = lax.ppermute(x, 'gz_1', [(1, 0)])  11.8 us
    pallas_call x2, Pallas kernels, update_rows(): pl.pallas_call(lambda *refs: update_kernel(start, count, *refs), out_shap...  5.91 us
    ppermute x3, starting transfers between devices, moved(): received = lax.ppermute(x, AXES, [(d, d - 2) for d in range(2, DEVICES)])  4 us
    ppermute x3, starting transfers between devices, moved(): above = lax.ppermute(received, 'gz_1', [(0, 1)])  3.86 us
    pallas_call x1, Pallas kernels, shards(): pl.pallas_call(pack_kernel, out_shape=(jax.ShapeDtypeStruct((8, 1, BLOCK)...  2.82 us
  transfers between devices with their start and end apart: 9, of which 2 were waited for; matrix products, arithmetic and copies ran while one was open for 0% of the time, Pallas kernels for 4%

profile of v3, /device:TPU:1, one launch (start us, length us, event | category | flops | bytes accessed | tf_op | source)
XLA Modules:
  0.0 98.9 jit_solution(10575994412912468104)
XLA Ops:
  0.6 0.0 copy-start
  0.6 2.8 %pack.1 = (f32[8,1,128]{2,1,0:T(1,128)}, f32[105,2048]{1,0:T(8,128)}, f32[72,2048]{1,0:T(8,128)}) custom-call(f32[59,2048]{1,0:T(8,128)} %g_ref.1, f32[59,2048]{1,0:T(8,128)} %m_ref.1, f32[59,2048]{1,0:T(8,128)} %v_ref.1, s32[16,128]{1,0:T(8,128)} %bitcast.2), custom_call_target="tpu_custom_call" | custom-call | tf_op jit(solution)/shard_map/pack/pallas_call | solution.py:197
  3.5 0.0 copy-start.3
  3.5 1.4 %collective-permute-start.7 = (f32[105,2048]{1,0:T(8,128)}, f32[105,2048]{1,0:T(8,128)S(1)}, u32[]{:S(2)}, u32[]{:S(2)}) collective-permute-start(f32[105,2048]{1,0:T(8,128)} %get-tuple-element.20.refs_6_), channel_id=1, source_target_pairs={{2,0},{3,1},{4,2},{5,3},{6,4},{7,5},{8,6},{9,7},{10,8},{11,9},{12,... | collective-permute-start | bytes 2580488 | tf_op jit(solution)/shard_map/ppermute | solution.py:192
  4.9 1.3 %collective-permute-start.4 = (f32[72,2048]{1,0:T(8,128)}, f32[72,2048]{1,0:T(8,128)S(1)}, u32[]{:S(2)}, u32[]{:S(2)}) collective-permute-start(f32[72,2048]{1,0:T(8,128)} %get-tuple-element.19.refs_6_), channel_id=1, source_target_pairs={{2,0},{3,1},{4,2},{5,3},{6,4},{7,5},{8,6},{9,7},{10,8},{11,9},{12,... | collective-permute-start | bytes 1769480 | tf_op jit(solution)/shard_map/ppermute | solution.py:192
  6.2 0.0 copy-done
  6.2 1.3 %collective-permute-start.1 = (f32[59,2048]{1,0:T(8,128)S(1)}, f32[59,2048]{1,0:T(8,128)S(1)}, u32[]{:S(2)}, u32[]{:S(2)}) collective-permute-start(f32[59,2048]{1,0:T(8,128)S(1)} %copy-done), channel_id=1, source_target_pairs={{2,0},{3,1},{4,2},{5,3},{6,4},{7,5},{8,6},{9,7},{10,8},{11,9},{12,... | collective-permute-start | bytes 1449992 | tf_op jit(solution)/shard_map/ppermute | solution.py:192
  7.5 5.1 %collective-permute-start = (f32[59,2048]{1,0:T(8,128)S(1)}, f32[59,2048]{1,0:T(8,128)S(1)}, u32[]{:S(2)}, u32[]{:S(2)}) collective-permute-start(f32[59,2048]{1,0:T(8,128)S(1)} %copy-done), channel_id=1, source_target_pairs={{1,0},{3,2},{5,4},{7,6},{9,8},{11,10},{13,12},{15,14},{17,16},{19,... | collective-permute-start | bytes 1449992 | tf_op jit(solution)/shard_map/ppermute | solution.py:193
  12.6 1.3 %collective-permute-start.6 = (f32[105,2048]{1,0:T(8,128)}, f32[105,2048]{1,0:T(8,128)S(1)}, u32[]{:S(2)}, u32[]{:S(2)}) collective-permute-start(f32[105,2048]{1,0:T(8,128)} %get-tuple-element.20.refs_6_), channel_id=1, source_target_pairs={{1,0},{3,2},{5,4},{7,6},{9,8},{11,10},{13,12},{15,14},{17,16},{19,... | collective-permute-start | bytes 2580488 | tf_op jit(solution)/shard_map/ppermute | solution.py:193
  14.0 11.7 %collective-permute-done.7.refs_9_ = f32[105,2048]{1,0:T(8,128)S(1)} collective-permute-done((f32[105,2048]{1,0:T(8,128)}, f32[105,2048]{1,0:T(8,128)S(1)}, u32[]{:S(2)}, u32[]{:S(2)}) %collective-permute-start.7) | collective-permute-done | bytes 860192 | tf_op jit(solution)/shard_map/ppermute | solution.py:192
  25.7 1.3 %collective-permute-start.8 = (f32[105,2048]{1,0:T(8,128)S(1)}, f32[105,2048]{1,0:T(8,128)S(1)}, u32[]{:S(2)}, u32[]{:S(2)}) collective-permute-start(f32[105,2048]{1,0:T(8,128)S(1)} %collective-permute-done.7.refs_9_), channel_id=1, source_target_pairs={{0,1},{2,3},{4,5},{6,7},{8,9},{10,11},{12,13},{14,15},{16,17},{18,... | collective-permute-start | bytes 2580488 | tf_op jit(solution)/shard_map/ppermute | solution.py:194
  27.0 22.6 %collective-permute-done.1.refs_5_ = f32[59,2048]{1,0:T(8,128)S(1)} collective-permute-done((f32[59,2048]{1,0:T(8,128)S(1)}, f32[59,2048]{1,0:T(8,128)S(1)}, u32[]{:S(2)}, u32[]{:S(2)}) %collective-permute-start.1) | collective-permute-done | bytes 483360 | tf_op jit(solution)/shard_map/ppermute | solution.py:192
  49.6 5.3 %collective-permute-start.3 = (f32[72,2048]{1,0:T(8,128)}, f32[72,2048]{1,0:T(8,128)S(1)}, u32[]{:S(2)}, u32[]{:S(2)}) collective-permute-start(f32[72,2048]{1,0:T(8,128)} %get-tuple-element.19.refs_6_), channel_id=1, source_target_pairs={{1,0},{3,2},{5,4},{7,6},{9,8},{11,10},{13,12},{15,14},{17,16},{19,... | collective-permute-start | bytes 1769480 | tf_op jit(solution)/shard_map/ppermute | solution.py:193
  54.9 0.0 collective-permute-done.4.refs_9_
  54.9 1.3 %collective-permute-start.5 = (f32[72,2048]{1,0:T(8,128)S(1)}, f32[72,2048]{1,0:T(8,128)S(1)}, u32[]{:S(2)}, u32[]{:S(2)}) collective-permute-start(f32[72,2048]{1,0:T(8,128)S(1)} %collective-permute-done.4.refs_9_), channel_id=1, source_target_pairs={{0,1},{2,3},{4,5},{6,7},{8,9},{10,11},{12,13},{14,15},{16,17},{18,... | collective-permute-start | bytes 1769480 | tf_op jit(solution)/shard_map/ppermute | solution.py:194
  56.2 0.0 collective-permute-done.refs_3_
  56.2 1.3 %collective-permute-start.2 = (f32[59,2048]{1,0:T(8,128)S(1)}, f32[59,2048]{1,0:T(8,128)S(1)}, u32[]{:S(2)}, u32[]{:S(2)}) collective-permute-start(f32[59,2048]{1,0:T(8,128)S(1)} %collective-permute-done.1.refs_5_), channel_id=1, source_target_pairs={{0,1},{2,3},{4,5},{6,7},{8,9},{10,11},{12,13},{14,15},{16,17},{18,... | collective-permute-start | bytes 1449992 | tf_op jit(solution)/shard_map/ppermute | solution.py:194
  57.5 0.0 copy-done.3
  57.6 12.1 %all_to_all.10.near_ref = f32[8,1,128]{2,1,0:T(1,128)S(1)} all-to-all(f32[8,1,128]{2,1,0:T(1,128)S(1)} %copy-done.3), channel_id=1, replica_groups=mesh['gx'=8,'gy'=4,'gz_0'=4,'gz_1'=2] {'gz_0','gz_1'}, dimensions={0} | all-to-all | bytes 8192 | tf_op jit(solution)/shard_map/all_to_all | solution.py:208
  69.7 0.1 line.1
  69.8 21.3 %all_to_all.11.far_ref = f32[32,1,128]{2,1,0:T(1,128)S(1)} all-to-all(f32[32,1,128]{2,1,0:T(1,128)S(1)} %line.1), channel_id=1, replica_groups=mesh['gx'=8,'gy'=4,'gz_0'=4,'gz_1'=2] {'gx','gy'}, dimensions={0} | all-to-all | bytes 32768 | tf_op jit(solution)/shard_map/all_to_all | solution.py:215
  91.1 0.6 table.1
  91.7 0.0 collective-permute-done.6.refs_7_
  91.7 0.0 collective-permute-done.2.refs_4_
  91.7 0.0 collective-permute-done.8.refs_8_
  91.7 0.0 copy-start.1
  91.7 1.2 %copy-done.1 = f32[105,2048]{1,0:T(8,128)S(1)} copy-done((f32[105,2048]{1,0:T(8,128)S(1)}, f32[105,2048]{1,0:T(8,128)}, u32[]{:S(2)}) %copy-start.1) | copy-done | bytes 860184
  92.9 3.2 %update.2 = (f32[59,2048]{1,0:T(8,128)}, f32[59,2048]{1,0:T(8,128)}, f32[59,2048]{1,0:T(8,128)}) custom-call(s32[1,128]{1,0:T(1,128)S(1)} %get-tuple-element.17.refs_0_, f32[1,128]{1,0:T(1,128)S(1)} %get-tuple-element.18.refs_1_, f32[59,2048]{1,0:T(8,128)S(1)} %copy-done, f32[59,2048]{1,0:T(8,128)S(1)} %collective-permute-done.refs_3_, ...), custom_call_target="tpu_custom_call" | custom-call | flops 10000000 | bytes 2000000 | tf_op jit(solution)/shard_map/update/pallas_call | solution.py:167
  96.1 0.0 collective-permute-done.3.refs_7_
  96.1 0.0 collective-permute-done.5.refs_8_
  96.1 0.0 copy-done.2
  96.1 2.7 %update.3 = (f32[59,2048]{1,0:T(8,128)}, f32[59,2048]{1,0:T(8,128)}, f32[59,2048]{1,0:T(8,128)}) custom-call(s32[1,128]{1,0:T(1,128)S(1)} %get-tuple-element.17.refs_0_, f32[1,128]{1,0:T(1,128)S(1)} %get-tuple-element.18.refs_1_, f32[59,2048]{1,0:T(8,128)S(1)} %copy-done, ...), custom_call_target="tpu_custom_call", output_to_operand_aliasing={{0}: (10, {}), {1}: (11, {}), {2}: (12, {})} | custom-call | flops 10000000 | bytes 2000000 | tf_op jit(solution)/shard_map/update/pallas_call | solution.py:167
  (1 shorter events, 0.0 us)
Async XLA Ops:
  0.6 5.6 %copy-start = (f32[59,2048]{1,0:T(8,128)S(1)}, f32[59,2048]{1,0:T(8,128)}, u32[]{:S(2)}) copy-start(f32[59,2048]{1,0:T(8,128)} %refs_2_.3) | copy-start | bytes 1449988
  3.5 54.1 %copy-start.3 = (f32[8,1,128]{2,1,0:T(1,128)S(1)}, f32[8,1,128]{2,1,0:T(1,128)}, u32[]{:S(2)}) copy-start(f32[8,1,128]{2,1,0:T(1,128)} %get-tuple-element.16) | copy-start | bytes 12292
  3.5 22.3 %collective-permute-start.7 = (f32[105,2048]{1,0:T(8,128)}, f32[105,2048]{1,0:T(8,128)S(1)}, u32[]{:S(2)}, u32[]{:S(2)}) collective-permute-start(f32[105,2048]{1,0:T(8,128)} %get-tuple-element.20.refs_6_), channel_id=1, source_target_pairs={{2,0},{3,1},{4,2},{5,3},{6,4},{7,5},{8,6},{9,7},{10,8},{11,9},{12,... | collective-permute-start | bytes 2580488 | tf_op jit(solution)/shard_map/ppermute | solution.py:192
  4.9 50.0 %collective-permute-start.4 = (f32[72,2048]{1,0:T(8,128)}, f32[72,2048]{1,0:T(8,128)S(1)}, u32[]{:S(2)}, u32[]{:S(2)}) collective-permute-start(f32[72,2048]{1,0:T(8,128)} %get-tuple-element.19.refs_6_), channel_id=1, source_target_pairs={{2,0},{3,1},{4,2},{5,3},{6,4},{7,5},{8,6},{9,7},{10,8},{11,9},{12,... | collective-permute-start | bytes 1769480 | tf_op jit(solution)/shard_map/ppermute | solution.py:192
  6.2 43.4 %collective-permute-start.1 = (f32[59,2048]{1,0:T(8,128)S(1)}, f32[59,2048]{1,0:T(8,128)S(1)}, u32[]{:S(2)}, u32[]{:S(2)}) collective-permute-start(f32[59,2048]{1,0:T(8,128)S(1)} %copy-done), channel_id=1, source_target_pairs={{2,0},{3,1},{4,2},{5,3},{6,4},{7,5},{8,6},{9,7},{10,8},{11,9},{12,... | collective-permute-start | bytes 1449992 | tf_op jit(solution)/shard_map/ppermute | solution.py:192
  7.5 48.7 %collective-permute-start = (f32[59,2048]{1,0:T(8,128)S(1)}, f32[59,2048]{1,0:T(8,128)S(1)}, u32[]{:S(2)}, u32[]{:S(2)}) collective-permute-start(f32[59,2048]{1,0:T(8,128)S(1)} %copy-done), channel_id=1, source_target_pairs={{1,0},{3,2},{5,4},{7,6},{9,8},{11,10},{13,12},{15,14},{17,16},{19,... | collective-permute-start | bytes 1449992 | tf_op jit(solution)/shard_map/ppermute | solution.py:193
  12.6 79.1 %collective-permute-start.6 = (f32[105,2048]{1,0:T(8,128)}, f32[105,2048]{1,0:T(8,128)S(1)}, u32[]{:S(2)}, u32[]{:S(2)}) collective-permute-start(f32[105,2048]{1,0:T(8,128)} %get-tuple-element.20.refs_6_), channel_id=1, source_target_pairs={{1,0},{3,2},{5,4},{7,6},{9,8},{11,10},{13,12},{15,14},{17,16},{19,... | collective-permute-start | bytes 2580488 | tf_op jit(solution)/shard_map/ppermute | solution.py:193
  25.7 66.0 %collective-permute-start.8 = (f32[105,2048]{1,0:T(8,128)S(1)}, f32[105,2048]{1,0:T(8,128)S(1)}, u32[]{:S(2)}, u32[]{:S(2)}) collective-permute-start(f32[105,2048]{1,0:T(8,128)S(1)} %collective-permute-done.7.refs_9_), channel_id=1, source_target_pairs={{0,1},{2,3},{4,5},{6,7},{8,9},{10,11},{12,13},{14,15},{16,17},{18,... | collective-permute-start | bytes 2580488 | tf_op jit(solution)/shard_map/ppermute | solution.py:194
  49.6 46.5 %collective-permute-start.3 = (f32[72,2048]{1,0:T(8,128)}, f32[72,2048]{1,0:T(8,128)S(1)}, u32[]{:S(2)}, u32[]{:S(2)}) collective-permute-start(f32[72,2048]{1,0:T(8,128)} %get-tuple-element.19.refs_6_), channel_id=1, source_target_pairs={{1,0},{3,2},{5,4},{7,6},{9,8},{11,10},{13,12},{15,14},{17,16},{19,... | collective-permute-start | bytes 1769480 | tf_op jit(solution)/shard_map/ppermute | solution.py:193
  54.9 41.2 %collective-permute-start.5 = (f32[72,2048]{1,0:T(8,128)S(1)}, f32[72,2048]{1,0:T(8,128)S(1)}, u32[]{:S(2)}, u32[]{:S(2)}) collective-permute-start(f32[72,2048]{1,0:T(8,128)S(1)} %collective-permute-done.4.refs_9_), channel_id=1, source_target_pairs={{0,1},{2,3},{4,5},{6,7},{8,9},{10,11},{12,13},{14,15},{16,17},{18,... | collective-permute-start | bytes 1769480 | tf_op jit(solution)/shard_map/ppermute | solution.py:194
  56.2 35.5 %collective-permute-start.2 = (f32[59,2048]{1,0:T(8,128)S(1)}, f32[59,2048]{1,0:T(8,128)S(1)}, u32[]{:S(2)}, u32[]{:S(2)}) collective-permute-start(f32[59,2048]{1,0:T(8,128)S(1)} %collective-permute-done.1.refs_5_), channel_id=1, source_target_pairs={{0,1},{2,3},{4,5},{6,7},{8,9},{10,11},{12,13},{14,15},{16,17},{18,... | collective-permute-start | bytes 1449992 | tf_op jit(solution)/shard_map/ppermute | solution.py:194
  91.7 1.2 %copy-start.1 = (f32[105,2048]{1,0:T(8,128)S(1)}, f32[105,2048]{1,0:T(8,128)}, u32[]{:S(2)}) copy-start(f32[105,2048]{1,0:T(8,128)} %get-tuple-element.20.refs_6_) | copy-start | bytes 2580484
  92.9 3.2 %copy-start.2 = (f32[72,2048]{1,0:T(8,128)S(1)}, f32[72,2048]{1,0:T(8,128)}, u32[]{:S(2)}) copy-start(f32[72,2048]{1,0:T(8,128)} %get-tuple-element.19.refs_6_) | copy-start | bytes 1769476

commit v4 on v3

--- a/solution.py
+++ b/solution.py
@@ -15,7 +15,8 @@
 AXES = ("gx", "gy", "gz_0", "gz_1")
 NEAR = ("gz_0", "gz_1")
 FAR = ("gx", "gy")
-CHUNKS = ((24, 35), (0, 24))
+CHUNKS = ((32, 27), (0, 32))
+LAST = "1"
 
 beta_one = 0.9
 beta_two = 0.999
@@ -111,7 +112,7 @@
 
 
 def update_kernel(start, count, place, clip, *refs):
-    p_parts, parts = refs[0:4], refs[4:8]
+    p_parts, parts = refs[0:5], refs[5:10]
     p_all, m_all, v_all, p_block, block, p_rows, m_rows, v_rows, sems, out_sems = refs[-10:]
     core = lax.axis_index("gz_1")
     rows = pl.ds(start, count)
@@ -123,17 +124,25 @@
             pltpu.make_async_copy(p_ref.at[rows, lanes], p_block.at[:, here], sems.at[1, slot]),
         )
 
-    for slot in range(BLOCKS):
-        at = jnp.maximum(place[0, slot] - 1, 0)
-        part = at // BLOCKS
-        lanes = pl.ds(pl.multiple_of((at % BLOCKS) * BLOCK, BLOCK), BLOCK)
-        cases = (part == 0, (part == 1) & (core == 0), (part == 1) & (core == 1), part == 2)
-        for condition, p_ref, ref in zip(cases, p_parts, parts):
-
-            @pl.when(condition)
-            def _(p_ref=p_ref, ref=ref, lanes=lanes, slot=slot):
-                for copy in copies(p_ref, ref, lanes, slot):
-                    copy.start()
+    def gather(below_above, received):
+        for slot in range(BLOCKS):
+            at = jnp.maximum(place[0, slot] - 1, 0)
+            part = at // BLOCKS
+            lanes = pl.ds(pl.multiple_of((at % BLOCKS) * BLOCK, BLOCK), BLOCK)
+            for which, source in enumerate((0, below_above, received)):
+
+                @pl.when(part == which)
+                def _(source=source, lanes=lanes, slot=slot):
+                    for copy in copies(p_parts[source], parts[source], lanes, slot):
+                        copy.start()
+
+    @pl.when(core == 0)
+    def _():
+        gather(1, 3)
+
+    @pl.when(core == 1)
+    def _():
+        gather(2, 4)
 
     factor = clip[0, 0]
     for slot in range(BLOCKS):
@@ -169,7 +178,7 @@
         out_shape=(out_type,) * 3,
         in_specs=[SMEM, SMEM] + [ANY] * (len(operands) - 2),
         out_specs=(ANY,) * 3,
-        input_output_aliases={10 + i: i for i in range(len(outs))},
+        input_output_aliases={12 + i: i for i in range(len(outs))},
         scratch_shapes=[
             pltpu.VMEM((count, width), jnp.float32),
             pltpu.VMEM((3 * count, width), jnp.float32),
@@ -188,11 +197,17 @@
     f32 = jnp.float32
     small = pltpu.CompilerParams(vmem_limit_bytes=1024 * 1024)
 
-    def moved(x):
-        received = lax.ppermute(x, AXES, [(d, d - 2) for d in range(2, DEVICES)])
+    def moved(name, x):
+        def sent(first, stride):
+            return lax.ppermute(x, AXES, [(d, d - 2) for d in range(first, DEVICES, stride)])
+
+        if name == LAST:
+            even, odd = sent(2, 2), sent(3, 2)
+        else:
+            even = odd = sent(2, 1)
         below = lax.ppermute(x, "gz_1", [(1, 0)])
-        above = lax.ppermute(received, "gz_1", [(0, 1)])
-        return x, below, above, received
+        above = lax.ppermute(even, "gz_1", [(0, 1)])
+        return x, below, above, even, odd
 
     pairs, *own = pl.pallas_call(
         pack_kernel,
@@ -225,10 +240,10 @@
     )(near, far)
 
     out_type = jax.ShapeDtypeStruct(params.shape, f32)
-    p_parts = moved(params)
+    p_parts = moved("p", params)
     outs = ()
     for i, (start, count) in enumerate(CHUNKS):
-        parts = moved(own[i])
+        parts = moved(str(i), own[i])
         outs = update_rows(start, count, place, clip, p_parts, parts, outs, out_type)
     return (*outs, rms.reshape(()))
 

time: 99.3 us -> 93.6 us (0.943)
  waiting for transfers between devices: 34.3 us -> 20.2 us
  starting transfers between devices: 19.7 us -> 32.1 us
  blocking collectives: 33.4 us -> 29.5 us
    ppermute x6 -> x7, waiting for transfers between devices: 34.3 us -> 20.2 us  [the longest x4 20.2 us: sent(): lax.ppermute(x, AXES, [(d, d - 2) for d in range(first, DEVICES, stride)])]
    ppermute x3, starting transfers between devices: 11.8 us -> 23.6 us  [moved(): below = lax.ppermute(x, 'gz_1', [(1, 0)])]
    all_to_all x1, blocking collectives: 12.1 us -> 10.1 us  [shards(): near = lax.all_to_all(pairs, NEAR, 0, 0, tiled=True)]
    all_to_all x1, blocking collectives: 21.3 us -> 19.4 us  [shards(): far = lax.all_to_all(lines, FAR, 0, 0, tiled=True)]
    ppermute x6 -> x7, starting transfers between devices: 7.86 us -> 8.57 us  [the longest x4 4.7 us: sent(): lax.ppermute(x, AXES, [(d, d - 2) for d in range(first, DEVICES, stride)])]
  transfers between devices with their start and end apart: 9 -> 10, of which waited for: 2 -> 1; matrix products, arithmetic and copies ran while one was open for 0% -> 0% of each run, Pallas kernels for 4% -> 4%
where the time goes in v4:
time: 93.6 us; the launch traced here: 93.1 us
  starting transfers between devices  32.1 us (34%)
  blocking collectives  29.5 us (32%)
  waiting for transfers between devices  20.2 us (22%)
  Pallas kernels  9.31 us (10%)
  local copies, waits for them, and re-layouts  1.12 us (1%)
    ppermute x3, starting transfers between devices, moved(): below = lax.ppermute(x, 'gz_1', [(1, 0)])  23.6 us
    ppermute x4, waiting for transfers between devices, sent(): lax.ppermute(x, AXES, [(d, d - 2) for d in range(first, DEVICES, stride)])  20.2 us
    all_to_all x1, blocking collectives, shards(): far = lax.all_to_all(lines, FAR, 0, 0, tiled=True)  19.4 us
    all_to_all x1, blocking collectives, shards(): near = lax.all_to_all(pairs, NEAR, 0, 0, tiled=True)  10.1 us
    pallas_call x2, Pallas kernels, update_rows(): pl.pallas_call(lambda *refs: update_kernel(start, count, *refs), out_shap...  5.82 us
    ppermute x4, starting transfers between devices, sent(): lax.ppermute(x, AXES, [(d, d - 2) for d in range(first, DEVICES, stride)])  4.7 us
    ppermute x3, starting transfers between devices, moved(): above = lax.ppermute(even, 'gz_1', [(0, 1)])  3.88 us
    pallas_call x1, Pallas kernels, shards(): pl.pallas_call(pack_kernel, out_shape=(jax.ShapeDtypeStruct((8, 1, BLOCK)...  2.77 us
  transfers between devices with their start and end apart: 10, of which 1 were waited for; matrix products, arithmetic and copies ran while one was open for 0% of the time, Pallas kernels for 4%

profile of v4, /device:TPU:1, one launch (start us, length us, event | category | flops | bytes accessed | tf_op | source)
XLA Modules:
  0.0 93.1 jit_solution(1050066539507717812)
XLA Ops:
  0.6 0.0 copy-start
  0.6 2.8 %pack.1 = (f32[8,1,128]{2,1,0:T(1,128)}, f32[81,2048]{1,0:T(8,128)}, f32[96,2048]{1,0:T(8,128)}) custom-call(f32[59,2048]{1,0:T(8,128)} %g_ref.1, f32[59,2048]{1,0:T(8,128)} %m_ref.1, f32[59,2048]{1,0:T(8,128)} %v_ref.1, s32[16,128]{1,0:T(8,128)} %bitcast.2), custom_call_target="tpu_custom_call" | custom-call | tf_op jit(solution)/shard_map/pack/pallas_call | solution.py:212
  3.4 0.8 collective-permute-start.4
  4.3 1.3 %collective-permute-start.8 = (f32[81,2048]{1,0:T(8,128)}, f32[81,2048]{1,0:T(8,128)S(1)}, u32[]{:S(2)}, u32[]{:S(2)}) collective-permute-start(f32[81,2048]{1,0:T(8,128)} %get-tuple-element.20.refs_7_), channel_id=1, source_target_pairs={{2,0},{3,1},{4,2},{5,3},{6,4},{7,5},{8,6},{9,7},{10,8},{11,9},{12,... | collective-permute-start | bytes 1990664 | tf_op jit(solution)/shard_map/ppermute | solution.py:202
  5.6 0.0 copy-done
  5.6 1.3 %collective-permute-start.1 = (f32[59,2048]{1,0:T(8,128)S(1)}, f32[59,2048]{1,0:T(8,128)S(1)}, u32[]{:S(2)}, u32[]{:S(2)}) collective-permute-start(f32[59,2048]{1,0:T(8,128)S(1)} %copy-done), channel_id=1, source_target_pairs={{2,0},{3,1},{4,2},{5,3},{6,4},{7,5},{8,6},{9,7},{10,8},{11,9},{12,... | collective-permute-start | bytes 1449992 | tf_op jit(solution)/shard_map/ppermute | solution.py:202
  6.9 5.7 %collective-permute-start = (f32[59,2048]{1,0:T(8,128)S(1)}, f32[59,2048]{1,0:T(8,128)S(1)}, u32[]{:S(2)}, u32[]{:S(2)}) collective-permute-start(f32[59,2048]{1,0:T(8,128)S(1)} %copy-done), channel_id=1, source_target_pairs={{1,0},{3,2},{5,4},{7,6},{9,8},{11,10},{13,12},{15,14},{17,16},{19,... | collective-permute-start | bytes 1449992 | tf_op jit(solution)/shard_map/ppermute | solution.py:208
  12.6 1.3 %collective-permute-start.7 = (f32[81,2048]{1,0:T(8,128)}, f32[81,2048]{1,0:T(8,128)S(1)}, u32[]{:S(2)}, u32[]{:S(2)}) collective-permute-start(f32[81,2048]{1,0:T(8,128)} %get-tuple-element.20.refs_7_), channel_id=1, source_target_pairs={{1,0},{3,2},{5,4},{7,6},{9,8},{11,10},{13,12},{15,14},{17,16},{19,... | collective-permute-start | bytes 1990664 | tf_op jit(solution)/shard_map/ppermute | solution.py:208
  13.9 20.2 %collective-permute-done.1.refs_5_.refs_6_ = f32[59,2048]{1,0:T(8,128)S(1)} collective-permute-done((f32[59,2048]{1,0:T(8,128)S(1)}, f32[59,2048]{1,0:T(8,128)S(1)}, u32[]{:S(2)}, u32[]{:S(2)}) %collective-permute-start.1) | collective-permute-done | bytes 483360 | tf_op jit(solution)/shard_map/ppermute | solution.py:202
  34.1 1.3 %collective-permute-start.6 = (f32[96,2048]{1,0:T(8,128)}, f32[96,2048]{1,0:T(8,128)S(1)}, u32[]{:S(2)}, u32[]{:S(2)}) collective-permute-start(f32[96,2048]{1,0:T(8,128)} %get-tuple-element.19.refs_7_), channel_id=1, source_target_pairs={{3,1},{5,3},{7,5},{9,7},{11,9},{13,11},{15,13},{17,15},{19,17},{21... | collective-permute-start | bytes 2359304 | tf_op jit(solution)/shard_map/ppermute | solution.py:202
  35.4 0.0 collective-permute-done.refs_3_
  35.4 16.5 %collective-permute-start.3 = (f32[96,2048]{1,0:T(8,128)}, f32[96,2048]{1,0:T(8,128)S(1)}, u32[]{:S(2)}, u32[]{:S(2)}) collective-permute-start(f32[96,2048]{1,0:T(8,128)} %get-tuple-element.19.refs_7_), channel_id=1, source_target_pairs={{1,0},{3,2},{5,4},{7,6},{9,8},{11,10},{13,12},{15,14},{17,16},{19,... | collective-permute-start | bytes 2359304 | tf_op jit(solution)/shard_map/ppermute | solution.py:208
  52.0 0.0 collective-permute-done.4.refs_10_
  52.0 1.3 %collective-permute-start.5 = (f32[96,2048]{1,0:T(8,128)S(1)}, f32[96,2048]{1,0:T(8,128)S(1)}, u32[]{:S(2)}, u32[]{:S(2)}) collective-permute-start(f32[96,2048]{1,0:T(8,128)S(1)} %collective-permute-done.4.refs_10_), channel_id=1, source_target_pairs={{0,1},{2,3},{4,5},{6,7},{8,9},{10,11},{12,13},{14,15},{16,17},{18,... | collective-permute-start | bytes 2359304 | tf_op jit(solution)/shard_map/ppermute | solution.py:209
  53.3 0.0 collective-permute-done.8.refs_10_.refs_11_
  53.3 1.3 %collective-permute-start.9 = (f32[81,2048]{1,0:T(8,128)S(1)}, f32[81,2048]{1,0:T(8,128)S(1)}, u32[]{:S(2)}, u32[]{:S(2)}) collective-permute-start(f32[81,2048]{1,0:T(8,128)S(1)} %collective-permute-done.8.refs_10_.refs_11_), channel_id=1, source_target_pairs={{0,1},{2,3},{4,5},{6,7},{8,9},{10,11},{12,13},{14,15},{16,17},{18,... | collective-permute-start | bytes 1990664 | tf_op jit(solution)/shard_map/ppermute | solution.py:209
  54.6 0.0 collective-permute-done.7.refs_8_
  54.6 1.3 %collective-permute-start.2 = (f32[59,2048]{1,0:T(8,128)S(1)}, f32[59,2048]{1,0:T(8,128)S(1)}, u32[]{:S(2)}, u32[]{:S(2)}) collective-permute-start(f32[59,2048]{1,0:T(8,128)S(1)} %collective-permute-done.1.refs_5_.refs_6_), channel_id=1, source_target_pairs={{0,1},{2,3},{4,5},{6,7},{8,9},{10,11},{12,13},{14,15},{16,17},{18,... | collective-permute-start | bytes 1449992 | tf_op jit(solution)/shard_map/ppermute | solution.py:209
  55.9 0.0 copy-done.3
  55.9 10.1 %all_to_all.10.near_ref = f32[8,1,128]{2,1,0:T(1,128)S(1)} all-to-all(f32[8,1,128]{2,1,0:T(1,128)S(1)} %copy-done.3), channel_id=1, replica_groups=mesh['gx'=8,'gy'=4,'gz_0'=4,'gz_1'=2] {'gz_0','gz_1'}, dimensions={0} | all-to-all | bytes 8192 | tf_op jit(solution)/shard_map/all_to_all | solution.py:223
  66.0 0.1 line.1
  66.1 19.4 %all_to_all.11.far_ref = f32[32,1,128]{2,1,0:T(1,128)S(1)} all-to-all(f32[32,1,128]{2,1,0:T(1,128)S(1)} %line.1), channel_id=1, replica_groups=mesh['gx'=8,'gy'=4,'gz_0'=4,'gz_1'=2] {'gx','gy'}, dimensions={0} | all-to-all | bytes 32768 | tf_op jit(solution)/shard_map/all_to_all | solution.py:230
  85.5 0.6 table.1
  86.2 0.0 collective-permute-done.2.refs_4_
  86.2 0.0 collective-permute-done.9.refs_9_
  86.2 1.1 %copy-done.2 = f32[81,2048]{1,0:T(8,128)S(1)} copy-done((f32[81,2048]{1,0:T(8,128)S(1)}, f32[81,2048]{1,0:T(8,128)}, u32[]{:S(2)}) %copy-start.2) | copy-done | bytes 663576
  87.3 3.0 %update.2 = (f32[59,2048]{1,0:T(8,128)}, f32[59,2048]{1,0:T(8,128)}, f32[59,2048]{1,0:T(8,128)}) custom-call(s32[1,128]{1,0:T(1,128)S(1)} %get-tuple-element.17.refs_0_, f32[1,128]{1,0:T(1,128)S(1)} %get-tuple-element.18.refs_1_, f32[59,2048]{1,0:T(8,128)S(1)} %copy-done, f32[59,2048]{1,0:T(8,128)S(1)} %collective-permute-done.refs_3_, ...), custom_call_target="tpu_custom_call" | custom-call | flops 10000000 | bytes 2000000 | tf_op jit(solution)/shard_map/update/pallas_call | solution.py:176
  90.3 0.0 collective-permute-done.6.refs_11_
  90.3 0.0 collective-permute-done.3.refs_8_
  90.3 0.0 collective-permute-done.5.refs_9_
  90.3 0.0 copy-done.1
  90.3 2.8 %update.3 = (f32[59,2048]{1,0:T(8,128)}, f32[59,2048]{1,0:T(8,128)}, f32[59,2048]{1,0:T(8,128)}) custom-call(s32[1,128]{1,0:T(1,128)S(1)} %get-tuple-element.17.refs_0_, f32[1,128]{1,0:T(1,128)S(1)} %get-tuple-element.18.refs_1_, f32[59,2048]{1,0:T(8,128)S(1)} %copy-done, ...), custom_call_target="tpu_custom_call", output_to_operand_aliasing={{0}: (12, {}), {1}: (13, {}), {2}: (14, {})} | custom-call | flops 10000000 | bytes 2000000 | tf_op jit(solution)/shard_map/update/pallas_call | solution.py:176
  (3 shorter events, 0.0 us)
Async XLA Ops:
  0.6 4.9 %copy-start = (f32[59,2048]{1,0:T(8,128)S(1)}, f32[59,2048]{1,0:T(8,128)}, u32[]{:S(2)}) copy-start(f32[59,2048]{1,0:T(8,128)} %refs_2_.3) | copy-start | bytes 1449988
  3.4 52.5 %copy-start.3 = (f32[8,1,128]{2,1,0:T(1,128)S(1)}, f32[8,1,128]{2,1,0:T(1,128)}, u32[]{:S(2)}) copy-start(f32[8,1,128]{2,1,0:T(1,128)} %get-tuple-element.16) | copy-start | bytes 12292
  3.4 48.5 %collective-permute-start.4 = (f32[96,2048]{1,0:T(8,128)}, f32[96,2048]{1,0:T(8,128)S(1)}, u32[]{:S(2)}, u32[]{:S(2)}) collective-permute-start(f32[96,2048]{1,0:T(8,128)} %get-tuple-element.19.refs_7_), channel_id=1, source_target_pairs={{2,0},{4,2},{6,4},{8,6},{10,8},{12,10},{14,12},{16,14},{18,16},{20... | collective-permute-start | bytes 2359304 | tf_op jit(solution)/shard_map/ppermute | solution.py:202
  4.3 49.0 %collective-permute-start.8 = (f32[81,2048]{1,0:T(8,128)}, f32[81,2048]{1,0:T(8,128)S(1)}, u32[]{:S(2)}, u32[]{:S(2)}) collective-permute-start(f32[81,2048]{1,0:T(8,128)} %get-tuple-element.20.refs_7_), channel_id=1, source_target_pairs={{2,0},{3,1},{4,2},{5,3},{6,4},{7,5},{8,6},{9,7},{10,8},{11,9},{12,... | collective-permute-start | bytes 1990664 | tf_op jit(solution)/shard_map/ppermute | solution.py:202
  5.6 28.6 %collective-permute-start.1 = (f32[59,2048]{1,0:T(8,128)S(1)}, f32[59,2048]{1,0:T(8,128)S(1)}, u32[]{:S(2)}, u32[]{:S(2)}) collective-permute-start(f32[59,2048]{1,0:T(8,128)S(1)} %copy-done), channel_id=1, source_target_pairs={{2,0},{3,1},{4,2},{5,3},{6,4},{7,5},{8,6},{9,7},{10,8},{11,9},{12,... | collective-permute-start | bytes 1449992 | tf_op jit(solution)/shard_map/ppermute | solution.py:202
  6.9 28.6 %collective-permute-start = (f32[59,2048]{1,0:T(8,128)S(1)}, f32[59,2048]{1,0:T(8,128)S(1)}, u32[]{:S(2)}, u32[]{:S(2)}) collective-permute-start(f32[59,2048]{1,0:T(8,128)S(1)} %copy-done), channel_id=1, source_target_pairs={{1,0},{3,2},{5,4},{7,6},{9,8},{11,10},{13,12},{15,14},{17,16},{19,... | collective-permute-start | bytes 1449992 | tf_op jit(solution)/shard_map/ppermute | solution.py:208
  12.6 42.0 %collective-permute-start.7 = (f32[81,2048]{1,0:T(8,128)}, f32[81,2048]{1,0:T(8,128)S(1)}, u32[]{:S(2)}, u32[]{:S(2)}) collective-permute-start(f32[81,2048]{1,0:T(8,128)} %get-tuple-element.20.refs_7_), channel_id=1, source_target_pairs={{1,0},{3,2},{5,4},{7,6},{9,8},{11,10},{13,12},{15,14},{17,16},{19,... | collective-permute-start | bytes 1990664 | tf_op jit(solution)/shard_map/ppermute | solution.py:208
  34.1 56.1 %collective-permute-start.6 = (f32[96,2048]{1,0:T(8,128)}, f32[96,2048]{1,0:T(8,128)S(1)}, u32[]{:S(2)}, u32[]{:S(2)}) collective-permute-start(f32[96,2048]{1,0:T(8,128)} %get-tuple-element.19.refs_7_), channel_id=1, source_target_pairs={{3,1},{5,3},{7,5},{9,7},{11,9},{13,11},{15,13},{17,15},{19,17},{21... | collective-permute-start | bytes 2359304 | tf_op jit(solution)/shard_map/ppermute | solution.py:202
  35.4 54.9 %collective-permute-start.3 = (f32[96,2048]{1,0:T(8,128)}, f32[96,2048]{1,0:T(8,128)S(1)}, u32[]{:S(2)}, u32[]{:S(2)}) collective-permute-start(f32[96,2048]{1,0:T(8,128)} %get-tuple-element.19.refs_7_), channel_id=1, source_target_pairs={{1,0},{3,2},{5,4},{7,6},{9,8},{11,10},{13,12},{15,14},{17,16},{19,... | collective-permute-start | bytes 2359304 | tf_op jit(solution)/shard_map/ppermute | solution.py:208
  52.0 38.3 %collective-permute-start.5 = (f32[96,2048]{1,0:T(8,128)S(1)}, f32[96,2048]{1,0:T(8,128)S(1)}, u32[]{:S(2)}, u32[]{:S(2)}) collective-permute-start(f32[96,2048]{1,0:T(8,128)S(1)} %collective-permute-done.4.refs_10_), channel_id=1, source_target_pairs={{0,1},{2,3},{4,5},{6,7},{8,9},{10,11},{12,13},{14,15},{16,17},{18,... | collective-permute-start | bytes 2359304 | tf_op jit(solution)/shard_map/ppermute | solution.py:209
  53.3 32.9 %collective-permute-start.9 = (f32[81,2048]{1,0:T(8,128)S(1)}, f32[81,2048]{1,0:T(8,128)S(1)}, u32[]{:S(2)}, u32[]{:S(2)}) collective-permute-start(f32[81,2048]{1,0:T(8,128)S(1)} %collective-permute-done.8.refs_10_.refs_11_), channel_id=1, source_target_pairs={{0,1},{2,3},{4,5},{6,7},{8,9},{10,11},{12,13},{14,15},{16,17},{18,... | collective-permute-start | bytes 1990664 | tf_op jit(solution)/shard_map/ppermute | solution.py:209
  54.6 31.6 %collective-permute-start.2 = (f32[59,2048]{1,0:T(8,128)S(1)}, f32[59,2048]{1,0:T(8,128)S(1)}, u32[]{:S(2)}, u32[]{:S(2)}) collective-permute-start(f32[59,2048]{1,0:T(8,128)S(1)} %collective-permute-done.1.refs_5_.refs_6_), channel_id=1, source_target_pairs={{0,1},{2,3},{4,5},{6,7},{8,9},{10,11},{12,13},{14,15},{16,17},{18,... | collective-permute-start | bytes 1449992 | tf_op jit(solution)/shard_map/ppermute | solution.py:209
  86.2 1.1 %copy-start.2 = (f32[81,2048]{1,0:T(8,128)S(1)}, f32[81,2048]{1,0:T(8,128)}, u32[]{:S(2)}) copy-start(f32[81,2048]{1,0:T(8,128)} %get-tuple-element.20.refs_7_) | copy-start | bytes 1990660
  87.3 3.0 %copy-start.1 = (f32[96,2048]{1,0:T(8,128)S(1)}, f32[96,2048]{1,0:T(8,128)}, u32[]{:S(2)}) copy-start(f32[96,2048]{1,0:T(8,128)} %get-tuple-element.19.refs_7_) | copy-start | bytes 2359300

commit v5 on v4

--- a/solution.py
+++ b/solution.py
@@ -10,6 +10,7 @@
 FEATURES = 59
 BLOCK = 128
 BLOCKS = 16
+HALF = 4
 STEP = 10
 DEVICES = 256
 AXES = ("gx", "gy", "gz_0", "gz_1")
@@ -145,10 +146,13 @@
         gather(2, 4)
 
     factor = clip[0, 0]
+    leaving = []
     for slot in range(BLOCKS):
         here = pl.ds(slot * BLOCK, BLOCK)
-        for copy in copies(p_parts[0], parts[0], pl.ds(0, BLOCK), slot):
-            copy.wait()
+        if slot % HALF == 0:
+            for ready in range(slot, slot + HALF):
+                for copy in copies(p_parts[0], parts[0], pl.ds(0, BLOCK), ready):
+                    copy.wait()
         second = block[2 * count : 3 * count, here]
         kept = (second > 0.0) & (place[0, slot] > 0)
         clipped = factor * block[0:count, here]
@@ -160,13 +164,15 @@
         p_rows[:, here] = jnp.where(kept, updated, 0.0)
         m_rows[:, here] = jnp.where(kept, first, 0.0)
         v_rows[:, here] = jnp.where(kept, second, 0.0)
-    done = [
-        pltpu.make_async_copy(rows_ref, whole.at[rows, :], out_sems.at[i])
-        for i, (rows_ref, whole) in enumerate(((p_rows, p_all), (m_rows, m_all), (v_rows, v_all)))
-    ]
-    for copy in done:
-        copy.start()
-    for copy in done:
+        if slot % HALF == HALF - 1:
+            columns = pl.ds((slot // HALF) * HALF * BLOCK, HALF * BLOCK)
+            for i, (mine, whole) in enumerate(((p_rows, p_all), (m_rows, m_all), (v_rows, v_all))):
+                copy = pltpu.make_async_copy(
+                    mine.at[:, columns], whole.at[rows, columns], out_sems.at[slot // HALF, i]
+                )
+                copy.start()
+                leaving.append(copy)
+    for copy in leaving:
         copy.wait()
 
 
@@ -184,7 +190,7 @@
             pltpu.VMEM((3 * count, width), jnp.float32),
             *[pltpu.VMEM((count, width), jnp.float32)] * 3,
             pltpu.SemaphoreType.DMA((2, BLOCKS)),
-            pltpu.SemaphoreType.DMA((3,)),
+            pltpu.SemaphoreType.DMA((BLOCKS // HALF, 3)),
         ],
         compiler_params=pltpu.CompilerParams(vmem_limit_bytes=8 * 1024 * 1024),
         cost_estimate=pl.CostEstimate(flops=10000000, bytes_accessed=2000000, transcendentals=0),

time: 93.6 us -> 93.1 us (level)
  no operation moved by 1% of the time
where the time goes in v5:
time: 93.1 us; the launch traced here: 92.6 us
  starting transfers between devices  32.1 us (34%)
  blocking collectives  29.5 us (32%)
  waiting for transfers between devices  20.2 us (22%)
  Pallas kernels  8.78 us (9%)
  local copies, waits for them, and re-layouts  1.12 us (1%)
    ppermute x3, starting transfers between devices, moved(): below = lax.ppermute(x, 'gz_1', [(1, 0)])  23.6 us
    ppermute x4, waiting for transfers between devices, sent(): lax.ppermute(x, AXES, [(d, d - 2) for d in range(first, DEVICES, stride)])  20.2 us
    all_to_all x1, blocking collectives, shards(): far = lax.all_to_all(lines, FAR, 0, 0, tiled=True)  19.4 us
    all_to_all x1, blocking collectives, shards(): near = lax.all_to_all(pairs, NEAR, 0, 0, tiled=True)  10.1 us
    pallas_call x2, Pallas kernels, update_rows(): pl.pallas_call(lambda *refs: update_kernel(start, count, *refs), out_shap...  5.29 us
    ppermute x4, starting transfers between devices, sent(): lax.ppermute(x, AXES, [(d, d - 2) for d in range(first, DEVICES, stride)])  4.7 us
    ppermute x3, starting transfers between devices, moved(): above = lax.ppermute(even, 'gz_1', [(0, 1)])  3.88 us
    pallas_call x1, Pallas kernels, shards(): pl.pallas_call(pack_kernel, out_shape=(jax.ShapeDtypeStruct((8, 1, BLOCK)...  2.77 us
  transfers between devices with their start and end apart: 10, of which 1 were waited for; matrix products, arithmetic and copies ran while one was open for 0% of the time, Pallas kernels for 4%

profile of v5, /device:TPU:1, one launch (start us, length us, event | category | flops | bytes accessed | tf_op | source)
XLA Modules:
  0.0 92.6 jit_solution(4185587597981709883)
XLA Ops:
  0.6 0.0 copy-start
  0.6 2.8 %pack.1 = (f32[8,1,128]{2,1,0:T(1,128)}, f32[81,2048]{1,0:T(8,128)}, f32[96,2048]{1,0:T(8,128)}) custom-call(f32[59,2048]{1,0:T(8,128)} %g_ref.1, f32[59,2048]{1,0:T(8,128)} %m_ref.1, f32[59,2048]{1,0:T(8,128)} %v_ref.1, s32[16,128]{1,0:T(8,128)} %bitcast.2), custom_call_target="tpu_custom_call" | custom-call | tf_op jit(solution)/shard_map/pack/pallas_call | solution.py:218
  3.4 0.8 collective-permute-start.4
  4.3 1.3 %collective-permute-start.8 = (f32[81,2048]{1,0:T(8,128)}, f32[81,2048]{1,0:T(8,128)S(1)}, u32[]{:S(2)}, u32[]{:S(2)}) collective-permute-start(f32[81,2048]{1,0:T(8,128)} %get-tuple-element.20.refs_7_), channel_id=1, source_target_pairs={{2,0},{3,1},{4,2},{5,3},{6,4},{7,5},{8,6},{9,7},{10,8},{11,9},{12,... | collective-permute-start | bytes 1990664 | tf_op jit(solution)/shard_map/ppermute | solution.py:208
  5.6 0.0 copy-done
  5.6 1.3 %collective-permute-start.1 = (f32[59,2048]{1,0:T(8,128)S(1)}, f32[59,2048]{1,0:T(8,128)S(1)}, u32[]{:S(2)}, u32[]{:S(2)}) collective-permute-start(f32[59,2048]{1,0:T(8,128)S(1)} %copy-done), channel_id=1, source_target_pairs={{2,0},{3,1},{4,2},{5,3},{6,4},{7,5},{8,6},{9,7},{10,8},{11,9},{12,... | collective-permute-start | bytes 1449992 | tf_op jit(solution)/shard_map/ppermute | solution.py:208
  6.9 5.7 %collective-permute-start = (f32[59,2048]{1,0:T(8,128)S(1)}, f32[59,2048]{1,0:T(8,128)S(1)}, u32[]{:S(2)}, u32[]{:S(2)}) collective-permute-start(f32[59,2048]{1,0:T(8,128)S(1)} %copy-done), channel_id=1, source_target_pairs={{1,0},{3,2},{5,4},{7,6},{9,8},{11,10},{13,12},{15,14},{17,16},{19,... | collective-permute-start | bytes 1449992 | tf_op jit(solution)/shard_map/ppermute | solution.py:214
  12.6 1.3 %collective-permute-start.7 = (f32[81,2048]{1,0:T(8,128)}, f32[81,2048]{1,0:T(8,128)S(1)}, u32[]{:S(2)}, u32[]{:S(2)}) collective-permute-start(f32[81,2048]{1,0:T(8,128)} %get-tuple-element.20.refs_7_), channel_id=1, source_target_pairs={{1,0},{3,2},{5,4},{7,6},{9,8},{11,10},{13,12},{15,14},{17,16},{19,... | collective-permute-start | bytes 1990664 | tf_op jit(solution)/shard_map/ppermute | solution.py:214
  13.9 20.2 %collective-permute-done.1.refs_5_.refs_6_ = f32[59,2048]{1,0:T(8,128)S(1)} collective-permute-done((f32[59,2048]{1,0:T(8,128)S(1)}, f32[59,2048]{1,0:T(8,128)S(1)}, u32[]{:S(2)}, u32[]{:S(2)}) %collective-permute-start.1) | collective-permute-done | bytes 483360 | tf_op jit(solution)/shard_map/ppermute | solution.py:208
  34.1 1.3 %collective-permute-start.6 = (f32[96,2048]{1,0:T(8,128)}, f32[96,2048]{1,0:T(8,128)S(1)}, u32[]{:S(2)}, u32[]{:S(2)}) collective-permute-start(f32[96,2048]{1,0:T(8,128)} %get-tuple-element.19.refs_7_), channel_id=1, source_target_pairs={{3,1},{5,3},{7,5},{9,7},{11,9},{13,11},{15,13},{17,15},{19,17},{21... | collective-permute-start | bytes 2359304 | tf_op jit(solution)/shard_map/ppermute | solution.py:208
  35.4 0.0 collective-permute-done.refs_3_
  35.4 16.5 %collective-permute-start.3 = (f32[96,2048]{1,0:T(8,128)}, f32[96,2048]{1,0:T(8,128)S(1)}, u32[]{:S(2)}, u32[]{:S(2)}) collective-permute-start(f32[96,2048]{1,0:T(8,128)} %get-tuple-element.19.refs_7_), channel_id=1, source_target_pairs={{1,0},{3,2},{5,4},{7,6},{9,8},{11,10},{13,12},{15,14},{17,16},{19,... | collective-permute-start | bytes 2359304 | tf_op jit(solution)/shard_map/ppermute | solution.py:214
  52.0 0.0 collective-permute-done.4.refs_10_
  52.0 1.3 %collective-permute-start.5 = (f32[96,2048]{1,0:T(8,128)S(1)}, f32[96,2048]{1,0:T(8,128)S(1)}, u32[]{:S(2)}, u32[]{:S(2)}) collective-permute-start(f32[96,2048]{1,0:T(8,128)S(1)} %collective-permute-done.4.refs_10_), channel_id=1, source_target_pairs={{0,1},{2,3},{4,5},{6,7},{8,9},{10,11},{12,13},{14,15},{16,17},{18,... | collective-permute-start | bytes 2359304 | tf_op jit(solution)/shard_map/ppermute | solution.py:215
  53.3 0.0 collective-permute-done.8.refs_10_.refs_11_
  53.3 1.3 %collective-permute-start.9 = (f32[81,2048]{1,0:T(8,128)S(1)}, f32[81,2048]{1,0:T(8,128)S(1)}, u32[]{:S(2)}, u32[]{:S(2)}) collective-permute-start(f32[81,2048]{1,0:T(8,128)S(1)} %collective-permute-done.8.refs_10_.refs_11_), channel_id=1, source_target_pairs={{0,1},{2,3},{4,5},{6,7},{8,9},{10,11},{12,13},{14,15},{16,17},{18,... | collective-permute-start | bytes 1990664 | tf_op jit(solution)/shard_map/ppermute | solution.py:215
  54.6 0.0 collective-permute-done.7.refs_8_
  54.6 1.3 %collective-permute-start.2 = (f32[59,2048]{1,0:T(8,128)S(1)}, f32[59,2048]{1,0:T(8,128)S(1)}, u32[]{:S(2)}, u32[]{:S(2)}) collective-permute-start(f32[59,2048]{1,0:T(8,128)S(1)} %collective-permute-done.1.refs_5_.refs_6_), channel_id=1, source_target_pairs={{0,1},{2,3},{4,5},{6,7},{8,9},{10,11},{12,13},{14,15},{16,17},{18,... | collective-permute-start | bytes 1449992 | tf_op jit(solution)/shard_map/ppermute | solution.py:215
  55.9 0.0 copy-done.3
  55.9 10.1 %all_to_all.10.near_ref = f32[8,1,128]{2,1,0:T(1,128)S(1)} all-to-all(f32[8,1,128]{2,1,0:T(1,128)S(1)} %copy-done.3), channel_id=1, replica_groups=mesh['gx'=8,'gy'=4,'gz_0'=4,'gz_1'=2] {'gz_0','gz_1'}, dimensions={0} | all-to-all | bytes 8192 | tf_op jit(solution)/shard_map/all_to_all | solution.py:229
  66.0 0.1 line.1
  66.1 19.4 %all_to_all.11.far_ref = f32[32,1,128]{2,1,0:T(1,128)S(1)} all-to-all(f32[32,1,128]{2,1,0:T(1,128)S(1)} %line.1), channel_id=1, replica_groups=mesh['gx'=8,'gy'=4,'gz_0'=4,'gz_1'=2] {'gx','gy'}, dimensions={0} | all-to-all | bytes 32768 | tf_op jit(solution)/shard_map/all_to_all | solution.py:236
  85.5 0.6 table.1
  86.2 0.0 collective-permute-done.2.refs_4_
  86.2 0.0 collective-permute-done.9.refs_9_
  86.2 1.1 %copy-done.2 = f32[81,2048]{1,0:T(8,128)S(1)} copy-done((f32[81,2048]{1,0:T(8,128)S(1)}, f32[81,2048]{1,0:T(8,128)}, u32[]{:S(2)}) %copy-start.2) | copy-done | bytes 663576
  87.3 2.7 %update.2 = (f32[59,2048]{1,0:T(8,128)}, f32[59,2048]{1,0:T(8,128)}, f32[59,2048]{1,0:T(8,128)}) custom-call(s32[1,128]{1,0:T(1,128)S(1)} %get-tuple-element.17.refs_0_, f32[1,128]{1,0:T(1,128)S(1)} %get-tuple-element.18.refs_1_, f32[59,2048]{1,0:T(8,128)S(1)} %copy-done, f32[59,2048]{1,0:T(8,128)S(1)} %collective-permute-done.refs_3_, ...), custom_call_target="tpu_custom_call" | custom-call | flops 10000000 | bytes 2000000 | tf_op jit(solution)/shard_map/update/pallas_call | solution.py:182
  90.0 0.0 collective-permute-done.6.refs_11_
  90.0 0.0 collective-permute-done.3.refs_8_
  90.0 0.0 collective-permute-done.5.refs_9_
  90.1 0.0 copy-done.1
  90.1 2.5 %update.3 = (f32[59,2048]{1,0:T(8,128)}, f32[59,2048]{1,0:T(8,128)}, f32[59,2048]{1,0:T(8,128)}) custom-call(s32[1,128]{1,0:T(1,128)S(1)} %get-tuple-element.17.refs_0_, f32[1,128]{1,0:T(1,128)S(1)} %get-tuple-element.18.refs_1_, f32[59,2048]{1,0:T(8,128)S(1)} %copy-done, ...), custom_call_target="tpu_custom_call", output_to_operand_aliasing={{0}: (12, {}), {1}: (13, {}), {2}: (14, {})} | custom-call | flops 10000000 | bytes 2000000 | tf_op jit(solution)/shard_map/update/pallas_call | solution.py:182
  (3 shorter events, 0.0 us)
Async XLA Ops:
  0.6 4.9 %copy-start = (f32[59,2048]{1,0:T(8,128)S(1)}, f32[59,2048]{1,0:T(8,128)}, u32[]{:S(2)}) copy-start(f32[59,2048]{1,0:T(8,128)} %refs_2_.3) | copy-start | bytes 1449988
  3.4 52.5 %copy-start.3 = (f32[8,1,128]{2,1,0:T(1,128)S(1)}, f32[8,1,128]{2,1,0:T(1,128)}, u32[]{:S(2)}) copy-start(f32[8,1,128]{2,1,0:T(1,128)} %get-tuple-element.16) | copy-start | bytes 12292
  3.4 48.5 %collective-permute-start.4 = (f32[96,2048]{1,0:T(8,128)}, f32[96,2048]{1,0:T(8,128)S(1)}, u32[]{:S(2)}, u32[]{:S(2)}) collective-permute-start(f32[96,2048]{1,0:T(8,128)} %get-tuple-element.19.refs_7_), channel_id=1, source_target_pairs={{2,0},{4,2},{6,4},{8,6},{10,8},{12,10},{14,12},{16,14},{18,16},{20... | collective-permute-start | bytes 2359304 | tf_op jit(solution)/shard_map/ppermute | solution.py:208
  4.3 49.0 %collective-permute-start.8 = (f32[81,2048]{1,0:T(8,128)}, f32[81,2048]{1,0:T(8,128)S(1)}, u32[]{:S(2)}, u32[]{:S(2)}) collective-permute-start(f32[81,2048]{1,0:T(8,128)} %get-tuple-element.20.refs_7_), channel_id=1, source_target_pairs={{2,0},{3,1},{4,2},{5,3},{6,4},{7,5},{8,6},{9,7},{10,8},{11,9},{12,... | collective-permute-start | bytes 1990664 | tf_op jit(solution)/shard_map/ppermute | solution.py:208
  5.6 28.6 %collective-permute-start.1 = (f32[59,2048]{1,0:T(8,128)S(1)}, f32[59,2048]{1,0:T(8,128)S(1)}, u32[]{:S(2)}, u32[]{:S(2)}) collective-permute-start(f32[59,2048]{1,0:T(8,128)S(1)} %copy-done), channel_id=1, source_target_pairs={{2,0},{3,1},{4,2},{5,3},{6,4},{7,5},{8,6},{9,7},{10,8},{11,9},{12,... | collective-permute-start | bytes 1449992 | tf_op jit(solution)/shard_map/ppermute | solution.py:208
  6.9 28.6 %collective-permute-start = (f32[59,2048]{1,0:T(8,128)S(1)}, f32[59,2048]{1,0:T(8,128)S(1)}, u32[]{:S(2)}, u32[]{:S(2)}) collective-permute-start(f32[59,2048]{1,0:T(8,128)S(1)} %copy-done), channel_id=1, source_target_pairs={{1,0},{3,2},{5,4},{7,6},{9,8},{11,10},{13,12},{15,14},{17,16},{19,... | collective-permute-start | bytes 1449992 | tf_op jit(solution)/shard_map/ppermute | solution.py:214
  12.6 42.0 %collective-permute-start.7 = (f32[81,2048]{1,0:T(8,128)}, f32[81,2048]{1,0:T(8,128)S(1)}, u32[]{:S(2)}, u32[]{:S(2)}) collective-permute-start(f32[81,2048]{1,0:T(8,128)} %get-tuple-element.20.refs_7_), channel_id=1, source_target_pairs={{1,0},{3,2},{5,4},{7,6},{9,8},{11,10},{13,12},{15,14},{17,16},{19,... | collective-permute-start | bytes 1990664 | tf_op jit(solution)/shard_map/ppermute | solution.py:214
  34.1 55.9 %collective-permute-start.6 = (f32[96,2048]{1,0:T(8,128)}, f32[96,2048]{1,0:T(8,128)S(1)}, u32[]{:S(2)}, u32[]{:S(2)}) collective-permute-start(f32[96,2048]{1,0:T(8,128)} %get-tuple-element.19.refs_7_), channel_id=1, source_target_pairs={{3,1},{5,3},{7,5},{9,7},{11,9},{13,11},{15,13},{17,15},{19,17},{21... | collective-permute-start | bytes 2359304 | tf_op jit(solution)/shard_map/ppermute | solution.py:208
  35.4 54.6 %collective-permute-start.3 = (f32[96,2048]{1,0:T(8,128)}, f32[96,2048]{1,0:T(8,128)S(1)}, u32[]{:S(2)}, u32[]{:S(2)}) collective-permute-start(f32[96,2048]{1,0:T(8,128)} %get-tuple-element.19.refs_7_), channel_id=1, source_target_pairs={{1,0},{3,2},{5,4},{7,6},{9,8},{11,10},{13,12},{15,14},{17,16},{19,... | collective-permute-start | bytes 2359304 | tf_op jit(solution)/shard_map/ppermute | solution.py:214
  52.0 38.1 %collective-permute-start.5 = (f32[96,2048]{1,0:T(8,128)S(1)}, f32[96,2048]{1,0:T(8,128)S(1)}, u32[]{:S(2)}, u32[]{:S(2)}) collective-permute-start(f32[96,2048]{1,0:T(8,128)S(1)} %collective-permute-done.4.refs_10_), channel_id=1, source_target_pairs={{0,1},{2,3},{4,5},{6,7},{8,9},{10,11},{12,13},{14,15},{16,17},{18,... | collective-permute-start | bytes 2359304 | tf_op jit(solution)/shard_map/ppermute | solution.py:215
  53.3 32.9 %collective-permute-start.9 = (f32[81,2048]{1,0:T(8,128)S(1)}, f32[81,2048]{1,0:T(8,128)S(1)}, u32[]{:S(2)}, u32[]{:S(2)}) collective-permute-start(f32[81,2048]{1,0:T(8,128)S(1)} %collective-permute-done.8.refs_10_.refs_11_), channel_id=1, source_target_pairs={{0,1},{2,3},{4,5},{6,7},{8,9},{10,11},{12,13},{14,15},{16,17},{18,... | collective-permute-start | bytes 1990664 | tf_op jit(solution)/shard_map/ppermute | solution.py:215
  54.6 31.6 %collective-permute-start.2 = (f32[59,2048]{1,0:T(8,128)S(1)}, f32[59,2048]{1,0:T(8,128)S(1)}, u32[]{:S(2)}, u32[]{:S(2)}) collective-permute-start(f32[59,2048]{1,0:T(8,128)S(1)} %collective-permute-done.1.refs_5_.refs_6_), channel_id=1, source_target_pairs={{0,1},{2,3},{4,5},{6,7},{8,9},{10,11},{12,13},{14,15},{16,17},{18,... | collective-permute-start | bytes 1449992 | tf_op jit(solution)/shard_map/ppermute | solution.py:215
  86.2 1.1 %copy-start.2 = (f32[81,2048]{1,0:T(8,128)S(1)}, f32[81,2048]{1,0:T(8,128)}, u32[]{:S(2)}) copy-start(f32[81,2048]{1,0:T(8,128)} %get-tuple-element.20.refs_7_) | copy-start | bytes 1990660
  87.3 2.8 %copy-start.1 = (f32[96,2048]{1,0:T(8,128)S(1)}, f32[96,2048]{1,0:T(8,128)}, u32[]{:S(2)}) copy-start(f32[96,2048]{1,0:T(8,128)} %get-tuple-element.19.refs_7_) | copy-start | bytes 2359300

commit v6 on v5

--- a/solution.py
+++ b/solution.py
@@ -125,31 +125,47 @@
             pltpu.make_async_copy(p_ref.at[rows, lanes], p_block.at[:, here], sems.at[1, slot]),
         )
 
-    def gather(below_above, received):
-        for slot in range(BLOCKS):
+    def gather(first, below_above, received):
+        for slot in range(first, first + HALF):
             at = jnp.maximum(place[0, slot] - 1, 0)
-            part = at // BLOCKS
             lanes = pl.ds(pl.multiple_of((at % BLOCKS) * BLOCK, BLOCK), BLOCK)
-            for which, source in enumerate((0, below_above, received)):
-
-                @pl.when(part == which)
-                def _(source=source, lanes=lanes, slot=slot):
-                    for copy in copies(p_parts[source], parts[source], lanes, slot):
-                        copy.start()
-
-    @pl.when(core == 0)
-    def _():
-        gather(1, 3)
-
-    @pl.when(core == 1)
-    def _():
-        gather(2, 4)
-
+
+            def start(source, lanes=lanes, slot=slot):
+                for copy in copies(p_parts[source], parts[source], lanes, slot):
+                    copy.start()
+
+            @pl.when(at < BLOCKS)
+            def _(start=start):
+                start(0)
+
+            @pl.when(at >= BLOCKS)
+            def _(start=start, at=at):
+                @pl.when(at < 2 * BLOCKS)
+                def _():
+                    start(below_above)
+
+                @pl.when(at >= 2 * BLOCKS)
+                def _():
+                    start(received)
+
+    def gather_here(first):
+        @pl.when(core == 0)
+        def _():
+            gather(first, 1, 3)
+
+        @pl.when(core == 1)
+        def _():
+            gather(first, 2, 4)
+
+    gather_here(0)
+    gather_here(HALF)
     factor = clip[0, 0]
     leaving = []
     for slot in range(BLOCKS):
         here = pl.ds(slot * BLOCK, BLOCK)
         if slot % HALF == 0:
+            if 0 < slot < BLOCKS - HALF:
+                gather_here(slot + HALF)
             for ready in range(slot, slot + HALF):
                 for copy in copies(p_parts[0], parts[0], pl.ds(0, BLOCK), ready):
                     copy.wait()

time: 93.1 us -> 92.8 us (level)
  no operation moved by 1% of the time
where the time goes in v6:
time: 92.8 us; the launch traced here: 92.4 us
  starting transfers between devices  32.1 us (35%)
  blocking collectives  29.5 us (32%)
  waiting for transfers between devices  20.2 us (22%)
  Pallas kernels  8.53 us (9%)
  local copies, waits for them, and re-layouts  1.12 us (1%)
    ppermute x3, starting transfers between devices, moved(): below = lax.ppermute(x, 'gz_1', [(1, 0)])  23.6 us
    ppermute x4, waiting for transfers between devices, sent(): lax.ppermute(x, AXES, [(d, d - 2) for d in range(first, DEVICES, stride)])  20.2 us
    all_to_all x1, blocking collectives, shards(): far = lax.all_to_all(lines, FAR, 0, 0, tiled=True)  19.4 us
    all_to_all x1, blocking collectives, shards(): near = lax.all_to_all(pairs, NEAR, 0, 0, tiled=True)  10.1 us
    pallas_call x2, Pallas kernels, update_rows(): pl.pallas_call(lambda *refs: update_kernel(start, count, *refs), out_shap...  5.04 us
    ppermute x4, starting transfers between devices, sent(): lax.ppermute(x, AXES, [(d, d - 2) for d in range(first, DEVICES, stride)])  4.7 us
    ppermute x3, starting transfers between devices, moved(): above = lax.ppermute(even, 'gz_1', [(0, 1)])  3.88 us
    pallas_call x1, Pallas kernels, shards(): pl.pallas_call(pack_kernel, out_shape=(jax.ShapeDtypeStruct((8, 1, BLOCK)...  2.77 us
  transfers between devices with their start and end apart: 10, of which 1 were waited for; matrix products, arithmetic and copies ran while one was open for 0% of the time, Pallas kernels for 4%

profile of v6, /device:TPU:1, one launch (start us, length us, event | category | flops | bytes accessed | tf_op | source)
XLA Modules:
  0.0 92.4 jit_solution(11703985848741112213)
XLA Ops:
  0.6 0.0 copy-start
  0.6 2.8 %pack.1 = (f32[8,1,128]{2,1,0:T(1,128)}, f32[81,2048]{1,0:T(8,128)}, f32[96,2048]{1,0:T(8,128)}) custom-call(f32[59,2048]{1,0:T(8,128)} %g_ref.1, f32[59,2048]{1,0:T(8,128)} %m_ref.1, f32[59,2048]{1,0:T(8,128)} %v_ref.1, s32[16,128]{1,0:T(8,128)} %bitcast.2), custom_call_target="tpu_custom_call" | custom-call | tf_op jit(solution)/shard_map/pack/pallas_call | solution.py:234
  3.4 0.8 collective-permute-start.4
  4.3 1.3 %collective-permute-start.8 = (f32[81,2048]{1,0:T(8,128)}, f32[81,2048]{1,0:T(8,128)S(1)}, u32[]{:S(2)}, u32[]{:S(2)}) collective-permute-start(f32[81,2048]{1,0:T(8,128)} %get-tuple-element.20.refs_7_), channel_id=1, source_target_pairs={{2,0},{3,1},{4,2},{5,3},{6,4},{7,5},{8,6},{9,7},{10,8},{11,9},{12,... | collective-permute-start | bytes 1990664 | tf_op jit(solution)/shard_map/ppermute | solution.py:224
  5.6 0.0 copy-done
  5.6 1.3 %collective-permute-start.1 = (f32[59,2048]{1,0:T(8,128)S(1)}, f32[59,2048]{1,0:T(8,128)S(1)}, u32[]{:S(2)}, u32[]{:S(2)}) collective-permute-start(f32[59,2048]{1,0:T(8,128)S(1)} %copy-done), channel_id=1, source_target_pairs={{2,0},{3,1},{4,2},{5,3},{6,4},{7,5},{8,6},{9,7},{10,8},{11,9},{12,... | collective-permute-start | bytes 1449992 | tf_op jit(solution)/shard_map/ppermute | solution.py:224
  6.9 5.7 %collective-permute-start = (f32[59,2048]{1,0:T(8,128)S(1)}, f32[59,2048]{1,0:T(8,128)S(1)}, u32[]{:S(2)}, u32[]{:S(2)}) collective-permute-start(f32[59,2048]{1,0:T(8,128)S(1)} %copy-done), channel_id=1, source_target_pairs={{1,0},{3,2},{5,4},{7,6},{9,8},{11,10},{13,12},{15,14},{17,16},{19,... | collective-permute-start | bytes 1449992 | tf_op jit(solution)/shard_map/ppermute | solution.py:230
  12.6 1.3 %collective-permute-start.7 = (f32[81,2048]{1,0:T(8,128)}, f32[81,2048]{1,0:T(8,128)S(1)}, u32[]{:S(2)}, u32[]{:S(2)}) collective-permute-start(f32[81,2048]{1,0:T(8,128)} %get-tuple-element.20.refs_7_), channel_id=1, source_target_pairs={{1,0},{3,2},{5,4},{7,6},{9,8},{11,10},{13,12},{15,14},{17,16},{19,... | collective-permute-start | bytes 1990664 | tf_op jit(solution)/shard_map/ppermute | solution.py:230
  13.9 20.2 %collective-permute-done.1.refs_5_.refs_6_ = f32[59,2048]{1,0:T(8,128)S(1)} collective-permute-done((f32[59,2048]{1,0:T(8,128)S(1)}, f32[59,2048]{1,0:T(8,128)S(1)}, u32[]{:S(2)}, u32[]{:S(2)}) %collective-permute-start.1) | collective-permute-done | bytes 483360 | tf_op jit(solution)/shard_map/ppermute | solution.py:224
  34.1 1.3 %collective-permute-start.6 = (f32[96,2048]{1,0:T(8,128)}, f32[96,2048]{1,0:T(8,128)S(1)}, u32[]{:S(2)}, u32[]{:S(2)}) collective-permute-start(f32[96,2048]{1,0:T(8,128)} %get-tuple-element.19.refs_7_), channel_id=1, source_target_pairs={{3,1},{5,3},{7,5},{9,7},{11,9},{13,11},{15,13},{17,15},{19,17},{21... | collective-permute-start | bytes 2359304 | tf_op jit(solution)/shard_map/ppermute | solution.py:224
  35.4 0.0 collective-permute-done.refs_3_
  35.4 16.5 %collective-permute-start.3 = (f32[96,2048]{1,0:T(8,128)}, f32[96,2048]{1,0:T(8,128)S(1)}, u32[]{:S(2)}, u32[]{:S(2)}) collective-permute-start(f32[96,2048]{1,0:T(8,128)} %get-tuple-element.19.refs_7_), channel_id=1, source_target_pairs={{1,0},{3,2},{5,4},{7,6},{9,8},{11,10},{13,12},{15,14},{17,16},{19,... | collective-permute-start | bytes 2359304 | tf_op jit(solution)/shard_map/ppermute | solution.py:230
  52.0 0.0 collective-permute-done.4.refs_10_
  52.0 1.3 %collective-permute-start.5 = (f32[96,2048]{1,0:T(8,128)S(1)}, f32[96,2048]{1,0:T(8,128)S(1)}, u32[]{:S(2)}, u32[]{:S(2)}) collective-permute-start(f32[96,2048]{1,0:T(8,128)S(1)} %collective-permute-done.4.refs_10_), channel_id=1, source_target_pairs={{0,1},{2,3},{4,5},{6,7},{8,9},{10,11},{12,13},{14,15},{16,17},{18,... | collective-permute-start | bytes 2359304 | tf_op jit(solution)/shard_map/ppermute | solution.py:231
  53.3 0.0 collective-permute-done.8.refs_10_.refs_11_
  53.3 1.3 %collective-permute-start.9 = (f32[81,2048]{1,0:T(8,128)S(1)}, f32[81,2048]{1,0:T(8,128)S(1)}, u32[]{:S(2)}, u32[]{:S(2)}) collective-permute-start(f32[81,2048]{1,0:T(8,128)S(1)} %collective-permute-done.8.refs_10_.refs_11_), channel_id=1, source_target_pairs={{0,1},{2,3},{4,5},{6,7},{8,9},{10,11},{12,13},{14,15},{16,17},{18,... | collective-permute-start | bytes 1990664 | tf_op jit(solution)/shard_map/ppermute | solution.py:231
  54.6 0.0 collective-permute-done.7.refs_8_
  54.6 1.3 %collective-permute-start.2 = (f32[59,2048]{1,0:T(8,128)S(1)}, f32[59,2048]{1,0:T(8,128)S(1)}, u32[]{:S(2)}, u32[]{:S(2)}) collective-permute-start(f32[59,2048]{1,0:T(8,128)S(1)} %collective-permute-done.1.refs_5_.refs_6_), channel_id=1, source_target_pairs={{0,1},{2,3},{4,5},{6,7},{8,9},{10,11},{12,13},{14,15},{16,17},{18,... | collective-permute-start | bytes 1449992 | tf_op jit(solution)/shard_map/ppermute | solution.py:231
  55.9 0.0 copy-done.3
  55.9 10.1 %all_to_all.10.near_ref = f32[8,1,128]{2,1,0:T(1,128)S(1)} all-to-all(f32[8,1,128]{2,1,0:T(1,128)S(1)} %copy-done.3), channel_id=1, replica_groups=mesh['gx'=8,'gy'=4,'gz_0'=4,'gz_1'=2] {'gz_0','gz_1'}, dimensions={0} | all-to-all | bytes 8192 | tf_op jit(solution)/shard_map/all_to_all | solution.py:245
  66.0 0.1 line.1
  66.1 19.4 %all_to_all.11.far_ref = f32[32,1,128]{2,1,0:T(1,128)S(1)} all-to-all(f32[32,1,128]{2,1,0:T(1,128)S(1)} %line.1), channel_id=1, replica_groups=mesh['gx'=8,'gy'=4,'gz_0'=4,'gz_1'=2] {'gx','gy'}, dimensions={0} | all-to-all | bytes 32768 | tf_op jit(solution)/shard_map/all_to_all | solution.py:252
  85.5 0.6 table.1
  86.2 0.0 collective-permute-done.2.refs_4_
  86.2 0.0 collective-permute-done.9.refs_9_
  86.2 1.1 %copy-done.2 = f32[81,2048]{1,0:T(8,128)S(1)} copy-done((f32[81,2048]{1,0:T(8,128)S(1)}, f32[81,2048]{1,0:T(8,128)}, u32[]{:S(2)}) %copy-start.2) | copy-done | bytes 663576
  87.3 2.6 %update.2 = (f32[59,2048]{1,0:T(8,128)}, f32[59,2048]{1,0:T(8,128)}, f32[59,2048]{1,0:T(8,128)}) custom-call(s32[1,128]{1,0:T(1,128)S(1)} %get-tuple-element.17.refs_0_, f32[1,128]{1,0:T(1,128)S(1)} %get-tuple-element.18.refs_1_, f32[59,2048]{1,0:T(8,128)S(1)} %copy-done, f32[59,2048]{1,0:T(8,128)S(1)} %collective-permute-done.refs_3_, ...), custom_call_target="tpu_custom_call" | custom-call | flops 10000000 | bytes 2000000 | tf_op jit(solution)/shard_map/update/pallas_call | solution.py:198
  89.9 0.0 collective-permute-done.6.refs_11_
  89.9 0.0 collective-permute-done.3.refs_8_
  89.9 0.0 collective-permute-done.5.refs_9_
  89.9 0.0 copy-done.1
  89.9 2.4 %update.3 = (f32[59,2048]{1,0:T(8,128)}, f32[59,2048]{1,0:T(8,128)}, f32[59,2048]{1,0:T(8,128)}) custom-call(s32[1,128]{1,0:T(1,128)S(1)} %get-tuple-element.17.refs_0_, f32[1,128]{1,0:T(1,128)S(1)} %get-tuple-element.18.refs_1_, f32[59,2048]{1,0:T(8,128)S(1)} %copy-done, ...), custom_call_target="tpu_custom_call", output_to_operand_aliasing={{0}: (12, {}), {1}: (13, {}), {2}: (14, {})} | custom-call | flops 10000000 | bytes 2000000 | tf_op jit(solution)/shard_map/update/pallas_call | solution.py:198
  (3 shorter events, 0.0 us)
Async XLA Ops:
  0.6 4.9 %copy-start = (f32[59,2048]{1,0:T(8,128)S(1)}, f32[59,2048]{1,0:T(8,128)}, u32[]{:S(2)}) copy-start(f32[59,2048]{1,0:T(8,128)} %refs_2_.3) | copy-start | bytes 1449988
  3.4 52.5 %copy-start.3 = (f32[8,1,128]{2,1,0:T(1,128)S(1)}, f32[8,1,128]{2,1,0:T(1,128)}, u32[]{:S(2)}) copy-start(f32[8,1,128]{2,1,0:T(1,128)} %get-tuple-element.16) | copy-start | bytes 12292
  3.4 48.5 %collective-permute-start.4 = (f32[96,2048]{1,0:T(8,128)}, f32[96,2048]{1,0:T(8,128)S(1)}, u32[]{:S(2)}, u32[]{:S(2)}) collective-permute-start(f32[96,2048]{1,0:T(8,128)} %get-tuple-element.19.refs_7_), channel_id=1, source_target_pairs={{2,0},{4,2},{6,4},{8,6},{10,8},{12,10},{14,12},{16,14},{18,16},{20... | collective-permute-start | bytes 2359304 | tf_op jit(solution)/shard_map/ppermute | solution.py:224
  4.3 49.0 %collective-permute-start.8 = (f32[81,2048]{1,0:T(8,128)}, f32[81,2048]{1,0:T(8,128)S(1)}, u32[]{:S(2)}, u32[]{:S(2)}) collective-permute-start(f32[81,2048]{1,0:T(8,128)} %get-tuple-element.20.refs_7_), channel_id=1, source_target_pairs={{2,0},{3,1},{4,2},{5,3},{6,4},{7,5},{8,6},{9,7},{10,8},{11,9},{12,... | collective-permute-start | bytes 1990664 | tf_op jit(solution)/shard_map/ppermute | solution.py:224
  5.6 28.6 %collective-permute-start.1 = (f32[59,2048]{1,0:T(8,128)S(1)}, f32[59,2048]{1,0:T(8,128)S(1)}, u32[]{:S(2)}, u32[]{:S(2)}) collective-permute-start(f32[59,2048]{1,0:T(8,128)S(1)} %copy-done), channel_id=1, source_target_pairs={{2,0},{3,1},{4,2},{5,3},{6,4},{7,5},{8,6},{9,7},{10,8},{11,9},{12,... | collective-permute-start | bytes 1449992 | tf_op jit(solution)/shard_map/ppermute | solution.py:224
  6.9 28.6 %collective-permute-start = (f32[59,2048]{1,0:T(8,128)S(1)}, f32[59,2048]{1,0:T(8,128)S(1)}, u32[]{:S(2)}, u32[]{:S(2)}) collective-permute-start(f32[59,2048]{1,0:T(8,128)S(1)} %copy-done), channel_id=1, source_target_pairs={{1,0},{3,2},{5,4},{7,6},{9,8},{11,10},{13,12},{15,14},{17,16},{19,... | collective-permute-start | bytes 1449992 | tf_op jit(solution)/shard_map/ppermute | solution.py:230
  12.6 42.0 %collective-permute-start.7 = (f32[81,2048]{1,0:T(8,128)}, f32[81,2048]{1,0:T(8,128)S(1)}, u32[]{:S(2)}, u32[]{:S(2)}) collective-permute-start(f32[81,2048]{1,0:T(8,128)} %get-tuple-element.20.refs_7_), channel_id=1, source_target_pairs={{1,0},{3,2},{5,4},{7,6},{9,8},{11,10},{13,12},{15,14},{17,16},{19,... | collective-permute-start | bytes 1990664 | tf_op jit(solution)/shard_map/ppermute | solution.py:230
  34.1 55.8 %collective-permute-start.6 = (f32[96,2048]{1,0:T(8,128)}, f32[96,2048]{1,0:T(8,128)S(1)}, u32[]{:S(2)}, u32[]{:S(2)}) collective-permute-start(f32[96,2048]{1,0:T(8,128)} %get-tuple-element.19.refs_7_), channel_id=1, source_target_pairs={{3,1},{5,3},{7,5},{9,7},{11,9},{13,11},{15,13},{17,15},{19,17},{21... | collective-permute-start | bytes 2359304 | tf_op jit(solution)/shard_map/ppermute | solution.py:224
  35.4 54.5 %collective-permute-start.3 = (f32[96,2048]{1,0:T(8,128)}, f32[96,2048]{1,0:T(8,128)S(1)}, u32[]{:S(2)}, u32[]{:S(2)}) collective-permute-start(f32[96,2048]{1,0:T(8,128)} %get-tuple-element.19.refs_7_), channel_id=1, source_target_pairs={{1,0},{3,2},{5,4},{7,6},{9,8},{11,10},{13,12},{15,14},{17,16},{19,... | collective-permute-start | bytes 2359304 | tf_op jit(solution)/shard_map/ppermute | solution.py:230
  52.0 38.0 %collective-permute-start.5 = (f32[96,2048]{1,0:T(8,128)S(1)}, f32[96,2048]{1,0:T(8,128)S(1)}, u32[]{:S(2)}, u32[]{:S(2)}) collective-permute-start(f32[96,2048]{1,0:T(8,128)S(1)} %collective-permute-done.4.refs_10_), channel_id=1, source_target_pairs={{0,1},{2,3},{4,5},{6,7},{8,9},{10,11},{12,13},{14,15},{16,17},{18,... | collective-permute-start | bytes 2359304 | tf_op jit(solution)/shard_map/ppermute | solution.py:231
  53.3 32.9 %collective-permute-start.9 = (f32[81,2048]{1,0:T(8,128)S(1)}, f32[81,2048]{1,0:T(8,128)S(1)}, u32[]{:S(2)}, u32[]{:S(2)}) collective-permute-start(f32[81,2048]{1,0:T(8,128)S(1)} %collective-permute-done.8.refs_10_.refs_11_), channel_id=1, source_target_pairs={{0,1},{2,3},{4,5},{6,7},{8,9},{10,11},{12,13},{14,15},{16,17},{18,... | collective-permute-start | bytes 1990664 | tf_op jit(solution)/shard_map/ppermute | solution.py:231
  54.6 31.6 %collective-permute-start.2 = (f32[59,2048]{1,0:T(8,128)S(1)}, f32[59,2048]{1,0:T(8,128)S(1)}, u32[]{:S(2)}, u32[]{:S(2)}) collective-permute-start(f32[59,2048]{1,0:T(8,128)S(1)} %collective-permute-done.1.refs_5_.refs_6_), channel_id=1, source_target_pairs={{0,1},{2,3},{4,5},{6,7},{8,9},{10,11},{12,13},{14,15},{16,17},{18,... | collective-permute-start | bytes 1449992 | tf_op jit(solution)/shard_map/ppermute | solution.py:231
  86.2 1.1 %copy-start.2 = (f32[81,2048]{1,0:T(8,128)S(1)}, f32[81,2048]{1,0:T(8,128)}, u32[]{:S(2)}) copy-start(f32[81,2048]{1,0:T(8,128)} %get-tuple-element.20.refs_7_) | copy-start | bytes 1990660
  87.3 2.7 %copy-start.1 = (f32[96,2048]{1,0:T(8,128)S(1)}, f32[96,2048]{1,0:T(8,128)}, u32[]{:S(2)}) copy-start(f32[96,2048]{1,0:T(8,128)} %get-tuple-element.19.refs_7_) | copy-start | bytes 2359300
